TPU v7x, 32 devices: a whole 2x2x4 slice. The times are simulated.
32 devices in a mesh: groups: 2 (over y), dp: 4 (over z), tensor: 4 (over x, core).
Axes of the slice: x: 2, y: 2, z: 4, core: 2. Of those that a mesh axis runs over, the one named last changes fastest.
Arguments:
- patches: bfloat16 [8192, 1280], P(('groups', 'dp')), parts along dimension 0, may hold values from -64 to 64
- grids: int32 [8, 2], P(('groups', 'dp')), parts along dimension 0, may hold values from 16 to 32, as said below
- dest: int32 [8, 256], P(('groups', 'dp')), parts along dimension 0, may hold values from 0 to 1535, as said below
- norm_gain: float32 [1280], replicated, may hold values from 0.1 to 1.9
- qkv_weight: bfloat16 [3, 1280, 1280], P(None, None, 'tensor'), may hold values from -8 to 8
- qkv_bias: float32 [3, 1280], P(None, 'tensor'), may hold values from -3 to 3
- proj_weight: bfloat16 [1280, 1280], P('tensor'), may hold values from -0.15625 to 0.15625
- proj_bias: float32 [1280], replicated, may hold values from -3 to 3
- merge_gain: float32 [1280], replicated, may hold values from 0.1 to 1.9
- w_first: bfloat16 [5120, 5120], P('dp', 'tensor'), may hold values from -0.078125 to 0.078125
- b_first: float32 [5120], P('tensor'), may hold values from -3 to 3
- w_second: bfloat16 [5120, 8192], P('tensor', 'dp'), may hold values from -0.078125 to 0.078125
- b_second: float32 [8192], P('tensor'), may hold values from -3 to 3
- text_embed: bfloat16 [3072, 8192], P(('groups', 'dp'), 'tensor'), parts along dimension 0, may hold values from -6 to 6
Outputs:
- sequence: bfloat16 [3072, 8192], P(('groups', 'dp'), 'tensor'), parts along dimension 0
There are 2 independent parts, one for each index of `groups`. A program takes and returns all parts, laid end to end along the dimension named above; an argument that names none is the same for every part. Nothing has to cross between parts.
Inputs may be any that keep to these rules, and one draw needn't show every extreme that they name: `grids`: both sides of every grid are even, at least 16 and at most 32; in each part along `groups`, the first image (the one on dp index 0) has the full 32 x 32 grid. The rows dest[i, j] with j < grids[i, 0] * grids[i, 1] / 4 are distinct over all images; the live rows of one image reach at most 64 rows in each aligned block of 384 sequence rows, and exactly that many for a full grid.
All inputs are finite; a program needn't handle non-finite values.
Results may differ from a plain program's by a relative error of at most 0.014.
Values may be sent and summed in bfloat16 or wider, within the bound.
A program may use at most 128 MiB of HBM per device.

v0:
```python
import functools
import math

import jax
import jax.numpy as jnp
from jax import lax
from jax.experimental import pallas as pl
from jax.experimental.pallas import tpu as pltpu
from jax.sharding import PartitionSpec as P

MESH = pl.DeviceIdType.MESH

HEAD_DIM = 80
PATCHES = 1024
MERGED = 256


def rms_scale(values, gain):
    return values * lax.rsqrt(jnp.mean(values * values, axis=-1, keepdims=True) + 1e-06) * gain


def placement(dest, live_count, dp_count, seq_rows, capacity):
    merged_dev = dest.size
    live_rows = (jnp.arange(MERGED, dtype=jnp.int32)[None, :] < (live_count // 4)[:, None]).reshape(merged_dev)
    dest_flat = dest.reshape(merged_dev)
    shard_id = jnp.where(live_rows, dest_flat // seq_rows, dp_count)
    local_row = dest_flat % seq_rows
    index = jnp.arange(merged_dev, dtype=jnp.int32)
    earlier = (shard_id[:, None] == shard_id[None, :]) & (index[None, :] < index[:, None])
    rank = jnp.sum(earlier.astype(jnp.int32), axis=1)
    slot = jnp.where(live_rows & (rank < capacity), shard_id * capacity + rank, -1)
    hit = jnp.arange(dp_count * capacity, dtype=jnp.int32)[:, None] == slot[None, :]
    rows = jnp.max(jnp.where(hit, local_row[None, :], -1), axis=1)
    return hit.astype(jnp.bfloat16), rows


def attention(patches, live_count, norm_gain, qkv_weight, qkv_bias, images_dev, heads_dev):
    normed = rms_scale(patches.astype(jnp.float32), norm_gain).astype(jnp.bfloat16)
    projected = (
        jnp.einsum("rv,jvc->jrc", normed, qkv_weight, preferred_element_type=jnp.float32)
        + qkv_bias[:, None, :]
    )
    projected = projected.astype(jnp.bfloat16).reshape(3, images_dev, PATCHES, heads_dev, HEAD_DIM)
    scores = jnp.einsum(
        "iqhd,ikhd->ihqk", projected[0], projected[1], preferred_element_type=jnp.float32
    ) / math.sqrt(HEAD_DIM)
    live_keys = jnp.arange(PATCHES, dtype=jnp.int32)[None, :] < live_count[:, None]
    scores = jnp.where(live_keys[:, None, None, :], scores, jnp.float32(-1e30))
    peak_score = jnp.max(scores, axis=-1, keepdims=True)
    exponent = jnp.exp(scores - peak_score)
    weights = (exponent / jnp.sum(exponent, axis=-1, keepdims=True)).astype(jnp.bfloat16)
    attended = jnp.einsum(
        "ihqk,ikhd->iqhd", weights, projected[2], preferred_element_type=jnp.float32
    )
    return attended.astype(jnp.bfloat16).reshape(patches.shape[0], heads_dev * HEAD_DIM)


def merger_kernel(
    n, x_hbm, w1_hbm, bias, permute, w2_hbm, out_hbm,
    x, w1, w2, part, from_left, from_right, total, slots, acc, out,
    load_sem, sum_send, sum_recv, hid_send, hid_recv,
):
    chunks, _, block, wide = part.shape
    me = lax.axis_index("dp")
    left, right = lax.max(me - 1, 0), lax.min(me + 1, n - 1)
    has_left, has_right = me > 0, me < n - 1
    inner = has_left & has_right

    loads = [
        pltpu.make_async_copy(a, b, load_sem.at[i])
        for i, (a, b) in enumerate(((x_hbm, x), (w1_hbm, w1), (w2_hbm, w2)))
    ]
    for load in loads:
        load.start()

    barrier = pltpu.get_barrier_semaphore()

    @pl.when(has_left)
    def _():
        pl.semaphore_signal(barrier, inc=1, device_id={"dp": left}, device_id_type=MESH)

    @pl.when(has_right)
    def _():
        pl.semaphore_signal(barrier, inc=1, device_id={"dp": right}, device_id_type=MESH)

    pl.semaphore_wait(barrier, has_left.astype(jnp.int32) + has_right.astype(jnp.int32))

    def sum_right(c, b):
        return pltpu.make_async_remote_copy(
            part.at[c, b], from_left.at[c, b], sum_send.at[0, c, b], sum_recv.at[0, c, b],
            device_id={"dp": right}, device_id_type=MESH)

    def sum_left(c, b):
        return pltpu.make_async_remote_copy(
            part.at[c, b], from_right.at[c, b], sum_send.at[1, c, b], sum_recv.at[1, c, b],
            device_id={"dp": left}, device_id_type=MESH)

    def hid_right(c, b):
        return pltpu.make_async_remote_copy(
            slots.at[c, b], slots.at[c, b], hid_send.at[0, c, b], hid_recv.at[0, c, b],
            device_id={"dp": right}, device_id_type=MESH)

    def hid_left(c, b):
        return pltpu.make_async_remote_copy(
            slots.at[c, b], slots.at[c, b], hid_send.at[1, c, b], hid_recv.at[1, c, b],
            device_id={"dp": left}, device_id_type=MESH)

    def first(c):
        columns = pl.ds(pl.multiple_of(c * wide, wide), wide)

        def tile(b):
            part[c, b] = jnp.dot(
                x[pl.ds(pl.multiple_of(b * block, block), block), :], w1[:, columns],
                preferred_element_type=jnp.float32,
            ).astype(jnp.bfloat16)

        def up(i, carry):
            b = n - 1 - i
            tile(b)

            @pl.when((me == 0) & (b > 0))
            def _():
                sum_right(c, b).start()

            return carry

        def down(b, carry):
            tile(b)

            @pl.when((me == n - 1) & (b < n - 1))
            def _():
                sum_left(c, b).start()

            return carry

        @pl.when(me == 0)
        def _():
            lax.fori_loop(0, n, up, 0)

        @pl.when(me > 0)
        def _():
            lax.fori_loop(0, n, down, 0)

    def relay(c):
        def one(i, carry):
            b = n - 1 - i

            @pl.when(inner & (b > me))
            def _():
                sum_right(c, b).wait_recv()
                part[c, b] = (part[c, b].astype(jnp.float32) + from_left[c, b].astype(jnp.float32)).astype(jnp.bfloat16)
                sum_right(c, b).start()

            @pl.when(inner & (i < me))
            def _():
                sum_left(c, i).wait_recv()
                part[c, i] = (part[c, i].astype(jnp.float32) + from_right[c, i].astype(jnp.float32)).astype(jnp.bfloat16)
                sum_left(c, i).start()

            return carry

        lax.fori_loop(0, n, one, 0)

    def activate(c):
        total[...] = part[c, me].astype(jnp.float32) + bias[c]

        @pl.when(has_left)
        def _():
            sum_right(c, me).wait_recv()
            total[...] += from_left[c, me].astype(jnp.float32)

        @pl.when(has_right)
        def _():
            sum_left(c, me).wait_recv()
            total[...] += from_right[c, me].astype(jnp.float32)

        value = total[...]
        hidden = (0.5 * value * (1.0 + lax.erf(value * math.sqrt(0.5)))).astype(jnp.bfloat16)
        slots[c, me] = jnp.dot(permute[...], hidden, preferred_element_type=jnp.float32).astype(jnp.bfloat16)

        @pl.when(has_right)
        def _():
            hid_right(c, me).start()

        @pl.when(has_left)
        def _():
            hid_left(c, me).start()

    def spread(c):
        def one(k, carry):
            before, after = me - k, me + k

            @pl.when(before >= 0)
            def _():
                hid_right(c, before).wait_recv()

                @pl.when(has_right)
                def _():
                    hid_right(c, before).start()

            @pl.when(after < n)
            def _():
                hid_left(c, after).wait_recv()

                @pl.when(has_left)
                def _():
                    hid_left(c, after).start()

            return carry

        lax.fori_loop(1, n, one, 0)

    def second(c):
        depth = pl.ds(pl.multiple_of(c * wide, wide), wide)

        def one(b, carry):
            rows = pl.ds(pl.multiple_of(b * block, block), block)
            more = jnp.dot(slots[c, b], w2[depth, :], preferred_element_type=jnp.float32)

            @pl.when(c == 0)
            def _():
                acc[rows, :] = more

            @pl.when(c > 0)
            def _():
                acc[rows, :] += more

            return carry

        lax.fori_loop(0, n, one, 0)

    loads[0].wait()
    loads[1].wait()
    first(0)
    loads[2].wait()

    def step(s, carry):
        @pl.when(s + 1 < chunks)
        def _():
            first(s + 1)

        @pl.when(s < chunks)
        def _():
            relay(s)

        @pl.when((s >= 1) & (s <= chunks))
        def _():
            activate(s - 1)

        @pl.when(s >= 2)
        def _():
            spread(s - 2)
            second(s - 2)

        return carry

    lax.fori_loop(0, chunks + 2, step, 0)

    def finish(b, carry):
        rows = pl.ds(pl.multiple_of(b * block, block), block)
        out[rows, :] = acc[rows, :].astype(jnp.bfloat16)
        return carry

    lax.fori_loop(0, n, finish, 0)
    store = pltpu.make_async_copy(out, out_hbm, load_sem.at[0])
    store.start()

    def drain(c, carry):
        def one(b, inside):
            @pl.when(has_right & (b > me))
            def _():
                sum_right(c, b).wait_send()

            @pl.when(has_left & (b < me))
            def _():
                sum_left(c, b).wait_send()

            @pl.when(has_right & (b <= me))
            def _():
                hid_right(c, b).wait_send()

            @pl.when(has_left & (b >= me))
            def _():
                hid_left(c, b).wait_send()

            return inside

        return lax.fori_loop(0, n, one, carry)

    lax.fori_loop(0, chunks, drain, 0)
    store.wait()


def merger(x, w1, bias, permute, w2):
    n = lax.axis_size("dp")
    rows, depth = x.shape
    hidden, columns = w2.shape
    block = rows // n
    wide = 256 if hidden % 256 == 0 else 128
    chunks = hidden // wide
    any_space = pl.BlockSpec(memory_space=pl.ANY)
    vmem = pl.BlockSpec(memory_space=pltpu.VMEM)
    stack = pltpu.VMEM((chunks, n, block, wide), jnp.bfloat16)
    return pl.pallas_call(
        functools.partial(merger_kernel, n),
        out_shape=jax.ShapeDtypeStruct((rows, columns), jnp.bfloat16),
        in_specs=[any_space, any_space, vmem, vmem, any_space],
        out_specs=any_space,
        scratch_shapes=[
            pltpu.VMEM((rows, depth), jnp.bfloat16),
            pltpu.VMEM((depth, hidden), jnp.bfloat16),
            pltpu.VMEM((hidden, columns), jnp.bfloat16),
            stack,
            stack,
            stack,
            pltpu.VMEM((block, wide), jnp.float32),
            stack,
            pltpu.VMEM((rows, columns), jnp.float32),
            pltpu.VMEM((rows, columns), jnp.bfloat16),
            pltpu.SemaphoreType.DMA((3,)),
            pltpu.SemaphoreType.DMA((2, chunks, n)),
            pltpu.SemaphoreType.DMA((2, chunks, n)),
            pltpu.SemaphoreType.DMA((2, chunks, n)),
            pltpu.SemaphoreType.DMA((2, chunks, n)),
        ],
        compiler_params=pltpu.CompilerParams(
            collective_id=0, has_side_effects=True, vmem_limit_bytes=60 * 1024 * 1024
        ),
    )(x, w1, bias.reshape(chunks, 1, wide), permute, w2)


def place_kernel(
    n, y, out, half, across_sum, from_across, ready, landed, got,
    mate_send, mate_recv, across_send, across_recv, row_send, row_recv, end_send, end_recv,
):
    quarter = y.shape[3] // 4
    row, me = lax.axis_index("dp"), lax.axis_index("tensor")
    core, side = me % 2, me // 2
    mate, across = side * 2 + 1 - core, (1 - side) * 2 + core

    barrier = pltpu.get_barrier_semaphore()
    for k in range(1, 4):
        pl.semaphore_signal(barrier, inc=1, device_id={"tensor": (me + k) % 4}, device_id_type=MESH)
    for k in range(1, n):
        pl.semaphore_signal(barrier, inc=1, device_id={"dp": (row + k) % n}, device_id_type=MESH)
    pl.semaphore_wait(barrier, 3 + n - 1)

    def piece(index):
        return pl.ds(pl.multiple_of(index * quarter, quarter), quarter)

    def to_mate(i, j):
        return pltpu.make_async_remote_copy(
            y.at[i, :, :, piece((side + j) % 2 * 2 + 1 - core)], half.at[i, j], mate_send.at[i, j], mate_recv.at[i, j],
            device_id={"tensor": mate}, device_id_type=MESH)

    def to_across(i):
        return pltpu.make_async_remote_copy(
            across_sum.at[i], from_across.at[i], across_send.at[i], across_recv.at[i],
            device_id={"tensor": across}, device_id_type=MESH)

    def to_row(i, k):
        other = (row + k) % n
        return pltpu.make_async_remote_copy(
            ready.at[i, other], landed.at[row, i], row_send.at[i, k], row_recv.at[i, k],
            device_id={"dp": other}, device_id_type=MESH)

    def to_end(i, k, block):
        return pltpu.make_async_remote_copy(
            landed.at[block, i], got.at[me, i], end_send.at[i, k], end_recv.at[i, me],
            device_id={"tensor": block}, device_id_type=MESH)

    for i in range(n):
        for j in (1, 0):
            to_mate(i, j).start()

    for i in range(n):
        to_mate(i, 1).wait_recv()
        for s in range(n):
            across_sum[i, s] = (
                y[i, s, :, piece((1 - side) * 2 + core)].astype(jnp.float32) + half[i, 1, s].astype(jnp.float32)
            ).astype(jnp.bfloat16)
        to_across(i).start()

    for i in range(n):
        to_mate(i, 0).wait_recv()
        to_across(i).wait_recv()
        for s in range(n):
            ready[i, s] = (
                y[i, s, :, piece(me)].astype(jnp.float32)
                + half[i, 0, s].astype(jnp.float32)
                + from_across[i, s].astype(jnp.float32)
            ).astype(jnp.bfloat16)
        for k in range(1, n):
            to_row(i, k).start()
        landed[row, i] = ready[i, row]

    for i in range(n):
        for k in range(n):
            block = (row + n - k) % n
            if k:
                to_row(i, k).wait_recv()

            @pl.when(block == me)
            def _():
                got[me, i] = landed[block, i]

            @pl.when(block != me)
            def _():
                to_end(i, k, block).start()

    for i in range(n):
        for k in range(1, 4):
            other = (me + k) % 4
            pltpu.make_async_remote_copy(
                landed.at[0, i], got.at[other, i], end_send.at[i, 0], end_recv.at[i, other],
                device_id={"tensor": other}, device_id_type=MESH).wait_recv()
    for t in range(4):
        out[:, :, t * quarter:(t + 1) * quarter] = got[t]

    for i in range(n):
        for j in range(2):
            to_mate(i, j).wait_send()
        to_across(i).wait_send()
        for k in range(1, n):
            to_row(i, k).wait_send()
        for k in range(n):
            block = (row + n - k) % n

            @pl.when(block != me)
            def _():
                to_end(i, k, block).wait_send()


def place(second):
    n, _, capacity, columns = second.shape
    quarter = columns // 4
    vmem = pl.BlockSpec(memory_space=pltpu.VMEM)
    stack = pltpu.VMEM((n, n, capacity, quarter), jnp.bfloat16)
    return pl.pallas_call(
        functools.partial(place_kernel, n),
        out_shape=jax.ShapeDtypeStruct((n, capacity, columns), jnp.bfloat16),
        in_specs=[vmem],
        out_specs=vmem,
        scratch_shapes=[
            pltpu.VMEM((n, 2, n, capacity, quarter), jnp.bfloat16),
            stack,
            stack,
            stack,
            stack,
            stack,
            pltpu.SemaphoreType.DMA((n, 2)),
            pltpu.SemaphoreType.DMA((n, 2)),
            pltpu.SemaphoreType.DMA((n,)),
            pltpu.SemaphoreType.DMA((n,)),
            pltpu.SemaphoreType.DMA((n, n)),
            pltpu.SemaphoreType.DMA((n, n)),
            pltpu.SemaphoreType.DMA((n, n)),
            pltpu.SemaphoreType.DMA((n, n)),
        ],
        compiler_params=pltpu.CompilerParams(
            collective_id=1, has_side_effects=True, vmem_limit_bytes=40 * 1024 * 1024
        ),
    )(second)


def exchange(second, dp_count, tensor_count, capacity):
    if dp_count == tensor_count == 4 and capacity % 16 == 0 and second.shape[1] % 512 == 0:
        return place(second.reshape(dp_count, dp_count, capacity, -1)).reshape(dp_count * capacity, -1)
    second = lax.psum_scatter(second, "tensor", scatter_dimension=1, tiled=True)
    columns = second.shape[1]
    second = second.reshape(dp_count, dp_count, capacity, columns)
    second = lax.all_to_all(second, "dp", split_axis=1, concat_axis=0, tiled=False)
    blocks = dp_count // tensor_count
    second = second.reshape(tensor_count, blocks, dp_count * capacity, columns)
    second = lax.all_to_all(second, "tensor", split_axis=0, concat_axis=0, tiled=True)
    return second.transpose(2, 1, 0, 3).reshape(dp_count * capacity, -1)


def local(
    patches,
    grids,
    dest,
    norm_gain,
    qkv_weight,
    qkv_bias,
    proj_weight,
    proj_bias,
    merge_gain,
    w_first,
    b_first,
    w_second,
    b_second,
    text_embed,
):
    rows_dev, width = patches.shape
    images_dev = grids.shape[0]
    heads_dev = qkv_weight.shape[2] // HEAD_DIM
    dp_count = lax.axis_size("dp")
    tensor_count = lax.axis_size("tensor")
    seq_rows = text_embed.shape[0]
    capacity = images_dev * (MERGED // dp_count)
    live_count = grids[:, 0] * grids[:, 1]
    permute, slot_rows = placement(dest, live_count, dp_count, seq_rows, capacity)
    arrived_rows = lax.all_to_all(
        slot_rows.reshape(dp_count, capacity), "dp", split_axis=0, concat_axis=0, tiled=True
    ).reshape(-1)

    attended = attention(patches, live_count, norm_gain, qkv_weight, qkv_bias, images_dev, heads_dev)
    partial_value = jnp.dot(attended, proj_weight, preferred_element_type=jnp.float32).astype(jnp.bfloat16)
    summed = lax.psum_scatter(partial_value, "tensor", scatter_dimension=0, tiled=True).astype(jnp.float32)
    part = rows_dev // tensor_count
    own = lax.dynamic_slice_in_dim(patches, lax.axis_index("tensor") * part, part, 0)
    resid = own.astype(jnp.float32) + summed + proj_bias
    merged_in = rms_scale(resid, merge_gain).astype(jnp.bfloat16).reshape(part // 4, 4 * width)
    sliced = lax.all_to_all(
        merged_in.reshape(part // 4, dp_count, 4 * width // dp_count), "dp", split_axis=1, concat_axis=0, tiled=False
    )
    received = lax.all_gather(sliced, "tensor", axis=1, tiled=False)
    received = received.reshape(-1, 4 * width // dp_count)
    second = merger(received, w_first, b_first, permute, w_second)
    visual = exchange(second, dp_count, tensor_count, capacity)
    visual = (visual.astype(jnp.float32) + b_second).astype(jnp.bfloat16)
    hit = jnp.arange(seq_rows, dtype=jnp.int32)[:, None] == arrived_rows[None, :]
    placed = jnp.dot(hit.astype(jnp.bfloat16), visual, preferred_element_type=jnp.float32).astype(jnp.bfloat16)
    return jnp.where(jnp.any(hit, axis=1)[:, None], placed, text_embed)


def solution(mesh):
    in_specs = (
        P(("groups", "dp"), None),
        P(("groups", "dp"), None),
        P(("groups", "dp"), None),
        P(),
        P(None, None, "tensor"),
        P(None, "tensor"),
        P("tensor", None),
        P(),
        P(),
        P("dp", "tensor"),
        P("tensor"),
        P("tensor", "dp"),
        P("tensor"),
        P(("groups", "dp"), "tensor"),
    )
    out_specs = P(("groups", "dp"), "tensor")
    return jax.shard_map(local, mesh=mesh, in_specs=in_specs, out_specs=out_specs, check_vma=False)
```

profile of v0, /device:TPU:1, one launch (start us, length us, event | category | flops | bytes accessed | tf_op | source)
XLA Modules:
  0.0 288.4 jit_solution(2297866779915644670)
XLA Ops:
  6.5 0.0 copy-start
  6.5 0.0 copy-start.11
  6.5 0.0 copy-start.9
  6.5 0.0 reduce-scatter.2.cloned.1.call-start
  6.5 0.0 copy-start.2
  6.6 1.5 fusion.32
  8.0 2.4 fusion.6
  10.4 0.0 copy-done
  10.5 0.0 copy-done.11
  10.5 0.0 copy-done.9
  10.5 0.0 copy-done.2
  10.5 2.8 fusion.16
  13.3 1.3 fusion.31
  15.8 10.9 %fusion.33 = (f32[4,1024]{1,0:T(4,128)S(1)}, f32[4,1024,1024]{1,2,0:T(8,128)}) fusion(pred[1024]{0:T(1024)(128)(4,1)S(1)} %iota_compare_fusion.4, bf16[1024,4,80]{0,2,1:T(8,128)(2,1)} %bitcast.46, bf16[1024,4,80]{0,2,1:T(8,128)(2,1)} %bitcast.45), kind=kOutput, calls=%fused_computation.56 | convolution fusion | flops 687866880 | bytes 18105344 | tf_op jit(solution)/shard_map/sub | solution.py:50
  26.7 0.0 copy-start.8
  26.7 7.4 %fusion.21 = bf16[4,80,1024]{2,1,0:T(8,128)(2,1)S(1)} fusion(bf16[1024,4,80]{0,2,1:T(8,128)(2,1)S(1)} %bitcast.44, f32[4,1024,1024]{1,2,0:T(8,128)} %get-tuple-element.14, f32[4,1024]{1,0:T(4,128)S(1)} %get-tuple-element.13), kind=kOutput, calls=%fused_computation.26 | convolution fusion | flops 679804928 | bytes 18104320 | tf_op jit(solution)/shard_map/ihqk,ikhd->iqhd/dot_general | solution.py:52
  34.2 0.0 copy-done.8
  34.2 3.1 %convolution_convert_fusion = bf16[1024,1280]{1,0:T(8,128)(2,1)} fusion(bf16[1024,320]{0,1:T(8,128)(2,1)S(1)} %bitcast.53, bf16[320,1280]{1,0:T(8,128)(2,1)S(1)} %copy-done.8), kind=kOutput, calls=%fused_computation.15 | convolution fusion | flops 840171520 | bytes 4096000 | tf_op jit(solution)/shard_map/dot_general | solution.py:509
  37.2 0.0 copy-start.3
  37.2 0.0 copy-start.4
  37.2 0.0 reduce-scatter.2.cloned.1.call-update
  37.3 0.0 all-gather.3.cloned.1.call-start
  37.3 36.5 %reduce-scatter.2.cloned.1.call-done = bf16[256,1280]{1,0:T(8,128)(2,1)} async-done(((bf16[1024,1280]{1,0:T(8,128)(2,1)}), bf16[256,1280]{1,0:T(8,128)(2,1)}) %reduce-scatter.2.cloned.1.call-update) | async-done | bytes 655376 | tf_op jit(solution)/shard_map/reduce_scatter | solution.py:510
  73.8 0.0 copy-done.3
  73.8 1.6 multiply_reduce_fusion
  75.4 0.0 copy-done.4
  75.4 1.6 multiply_convert_fusion
  77.0 0.0 copy-start.6
  77.0 0.0 copy-start.5
  77.0 1.0 broadcast_in_dim_reshape_reshape.3
  78.0 1.2 copy.25
  79.2 20.5 %all_to_all.24 = bf16[1,64,4,1280]{3,1,0,2:T(8,128)(2,1)} all-to-all(bf16[1,64,4,1280]{3,1,0,2:T(8,128)(2,1)S(1)} %copy.25), channel_id=1, replica_groups=mesh['groups'=2,'dp'=4,'tensor'=4] {'dp'}, dimensions={2} | all-to-all | bytes 1310720 | tf_op jit(solution)/shard_map/all_to_all | solution.py:515
  99.7 0.0 all-gather.3.cloned.1.call-update
  99.8 0.0 copy-done.6
  99.9 0.2 convert_reduce_fusion
  100.1 0.1 select_reduce_fusion
  100.2 0.6 all_to_all.17
  100.8 3.3 %all-to-all-start = ((s32[4,1,64]{2,1,0:T(1,128)}), s32[4,1,64]{2,1,0:T(1,128)S(1)}, u32[]{:S(2)}, u32[]{:S(2)}) async-start(s32[4,1,64]{2,1,0:T(1,128)} %all_to_all.17), calls=%async_computation | async-start | bytes 4096 | tf_op jit(solution)/shard_map/all_to_all | solution.py:504
  104.1 0.7 fusion.25.permute
  104.8 0.0 copy-done.5
  104.8 0.6 reshape.163.bias
  105.4 3.0 %all-to-all-done = s32[4,1,64]{2,1,0:T(1,128)S(1)} async-done(((s32[4,1,64]{2,1,0:T(1,128)}), s32[4,1,64]{2,1,0:T(1,128)S(1)}, u32[]{:S(2)}, u32[]{:S(2)}) %all-to-all-start) | async-done | bytes 1056 | tf_op jit(solution)/shard_map/all_to_all | solution.py:504
  108.4 0.5 broadcast.138
  108.9 0.6 reduce.9
  109.4 0.1 eq.59
  109.5 0.2 fusion.24
  109.7 15.6 %all-gather.3.cloned.1.call-done = bf16[4,4,64,1,1280]{4,2,3,0,1:T(8,128)(2,1)} async-done(((bf16[4,1,64,1,1280]{4,2,3,0,1:T(8,128)(2,1)}), bf16[4,4,64,1,1280]{4,2,3,0,1:T(8,128)(2,1)}) %all-gather.3.cloned.1.call-update) | async-done | bytes 2621456 | tf_op jit(solution)/shard_map/all_gather | solution.py:518
  125.2 3.5 %copy.27 = bf16[4,4,64,1,1280]{4,2,1,0,3:T(8,128)(2,1)} copy(bf16[4,4,64,1,1280]{4,2,3,0,1:T(8,128)(2,1)} %all-gather.3.cloned.1.call-done) | data formatting | bytes 5242880 | tf_op jit(solution)/shard_map/all_gather | solution.py:518
  128.8 99.2 %shard_map.136 = bf16[1024,2048]{1,0:T(8,128)(2,1)} custom-call(bf16[1024,1280]{1,0:T(8,128)(2,1)} %bitcast.42, bf16[1280,1280]{1,0:T(8,128)(2,1)} %w1_hbm.1, f32[5,1,256]{2,1,0:T(1,128)} %reshape.163.bias, bf16[256,256]{1,0:T(8,128)(2,1)} %fusion.25.permute, bf16[1280,2048]{1,0:T(8,128)(2,1)} %w2_hbm.1), custom_call_target="tpu_custom_call" | custom-call | tf_op jit(solution)/shard_map/pallas_call | solution.py:304
  228.0 0.0 copy-start.1
  228.0 2.2 copy-done.1
  230.1 0.0 copy-start.7
  230.2 0.0 copy-start.10
  230.2 49.6 %shard_map.137 = bf16[4,64,2048]{2,1,0:T(8,128)(2,1)S(1)} custom-call(bf16[4,4,64,2048]{3,2,1,0:T(8,128)(2,1)S(1)} %bitcast.40), custom_call_target="tpu_custom_call" | custom-call | tf_op jit(solution)/shard_map/pallas_call | solution.py:439
  279.7 0.0 copy-done.7
  279.8 0.0 copy-done.10
  279.8 1.7 fusion.14
  (7 shorter events, 0.1 us)
Async XLA Ops:
  6.5 3.9 %copy-start = (bf16[3,1280,320]{1,2,0:T(8,128)(2,1)S(1)}, bf16[3,1280,320]{1,2,0:T(8,128)(2,1)}, u32[]{:S(2)}) copy-start(bf16[3,1280,320]{1,2,0:T(8,128)(2,1)} %param.18) | copy-start | bytes 7372804
  6.5 3.9 %copy-start.11 = (f32[3,320]{1,0:T(4,128)S(1)}, f32[3,320]{1,0:T(4,128)}, u32[]{:S(2)}) copy-start(f32[3,320]{1,0:T(4,128)} %param.19) | copy-start | bytes 11524
  6.5 3.9 %copy-start.9 = (f32[1280]{0:T(1024)S(1)}, f32[1280]{0:T(1024)}, u32[]{:S(2)}) copy-start(f32[1280]{0:T(1024)} %param.17) | copy-start | bytes 15364
  6.5 67.3 %reduce-scatter.2.cloned.1.call-start = ((), (), s32[]{:S(2)}) async-start(), calls=%async_computation.3 | async-start | bytes 3276800 | tf_op jit(solution)/shard_map/reduce_scatter | solution.py:510
  6.5 3.9 %copy-start.2 = (bf16[1024,1280]{1,0:T(8,128)(2,1)S(1)}, bf16[1024,1280]{1,0:T(8,128)(2,1)}, u32[]{:S(2)}) copy-start(bf16[1024,1280]{1,0:T(8,128)(2,1)} %param.14) | copy-start | bytes 7864324
  26.7 7.4 %copy-start.8 = (bf16[320,1280]{1,0:T(8,128)(2,1)S(1)}, bf16[320,1280]{1,0:T(8,128)(2,1)}, u32[]{:S(2)}) copy-start(bf16[320,1280]{1,0:T(8,128)(2,1)} %param.20) | copy-start | bytes 2457604
  37.2 36.6 %copy-start.3 = (f32[1280]{0:T(1024)S(1)}, f32[1280]{0:T(1024)}, u32[]{:S(2)}) copy-start(f32[1280]{0:T(1024)} %param.21) | copy-start | bytes 15364
  37.2 38.2 %copy-start.4 = (f32[1280]{0:T(1024)S(1)}, f32[1280]{0:T(1024)}, u32[]{:S(2)}) copy-start(f32[1280]{0:T(1024)} %param.22) | copy-start | bytes 15364
  37.3 88.0 %all-gather.3.cloned.1.call-start = ((), (), s32[]{:S(2)}) async-start(), calls=%async_computation.4 | async-start | bytes 3276800 | tf_op jit(solution)/shard_map/all_gather | solution.py:518
  77.0 22.8 %copy-start.6 = (s32[1,256]{1,0:T(1,128)S(1)}, s32[1,256]{1,0:T(1,128)}, u32[]{:S(2)}) copy-start(s32[1,256]{1,0:T(1,128)} %param.16) | copy-start | bytes 3076
  77.0 27.7 %copy-start.5 = (f32[1280]{0:T(1024)S(1)}, f32[1280]{0:T(1024)}, u32[]{:S(2)}) copy-start(f32[1280]{0:T(1024)} %param.24) | copy-start | bytes 15364
  100.8 7.5 %all-to-all-start = ((s32[4,1,64]{2,1,0:T(1,128)}), s32[4,1,64]{2,1,0:T(1,128)S(1)}, u32[]{:S(2)}, u32[]{:S(2)}) async-start(s32[4,1,64]{2,1,0:T(1,128)} %all_to_all.17), calls=%async_computation | async-start | bytes 4096 | tf_op jit(solution)/shard_map/all_to_all | solution.py:504
  228.0 2.2 copy-start.1
  230.1 49.6 %copy-start.7 = (bf16[384,2048]{1,0:T(8,128)(2,1)S(1)}, bf16[384,2048]{1,0:T(8,128)(2,1)}, u32[]{:S(2)}) copy-start(bf16[384,2048]{1,0:T(8,128)(2,1)} %param.27) | copy-start | bytes 4718596
  230.2 49.6 %copy-start.10 = (f32[2048]{0:T(1024)S(1)}, f32[2048]{0:T(1024)}, u32[]{:S(2)}) copy-start(f32[2048]{0:T(1024)} %param.26) | copy-start | bytes 24580
Sparse Core Ops, SparseCore 0:
  37.4 36.3 reduce-scatter.1
  99.9 25.3 all-gather.2
where the time goes:
time: 289 us; the launch traced here: 288 us
  Pallas kernels  149 us (52%)
  waiting for transfers between devices  55.1 us (19%)
  matrix products  26 us (9%)
  blocking collectives  20.5 us (7%)
  between operations  14.9 us (5%)
  local copies, waits for them, and re-layouts  12.5 us (4%)
  other arithmetic  7.38 us (3%)
  starting transfers between devices  3.32 us (1%)
    pallas_call x1, Pallas kernels, merger(): pl.pallas_call(functools.partial(merger_kernel, n), out_shape=jax.ShapeDt...  99.2 us
    pallas_call x1, Pallas kernels, place(): pl.pallas_call(functools.partial(place_kernel, n), out_shape=jax.ShapeDty...  49.6 us
    reduce_scatter x1, waiting for transfers between devices, local(): lax.psum_scatter(partial_value, 'tensor', scatter_dimension=0, tiled=True)  36.5 us
    all_to_all x1, blocking collectives, local(): lax.all_to_all(merged_in.reshape(part // 4, dp_count, 4 * width // dp_cou...  20.5 us
    all_gather x1, waiting for transfers between devices, local(): received = lax.all_gather(sliced, 'tensor', axis=1, tiled=False)  15.6 us
    sub x1, matrix products, attention(): exponent = jnp.exp(scores - peak_score)  10.9 us
    dot_general x1, matrix products, attention(): jnp.einsum('ihqk,ikhd->iqhd', weights, projected[2], preferred_element_ty...  7.43 us
  transfers between devices with their start and end apart: 3, of which 3 were waited for; matrix products, arithmetic and copies ran while one was open for 1% of the time, Pallas kernels for 0%

commit v1 on v0

--- a/solution.py
+++ b/solution.py
@@ -525,6 +525,596 @@
     return jnp.where(jnp.any(hit, axis=1)[:, None], placed, text_embed)
 
 
+def encode_kernel(
+    seq_rows, patches_hbm, grids, dest, gain, wqkv_hbm, bqkv, wproj_hbm, bproj, mgain, x_out, arrived,
+    patches, wqkv, wproj, target, normed, own_rows, qs, ks, vs, att_f32, att_out, att_in, slices, rows_tbl,
+    load_sem, tbl_send, tbl_recv, pm_send, pa_send, py_send, pd_send, p_recv, pd_recv,
+    att_send, att_recv, z_send, fm_send, fa_send, fx_send, x_recv,
+):
+    n, _, part, width = x_out.shape
+    nt, block, span = att_in.shape
+    rows = n * block
+    merged = dest.shape[1]
+    heads = qs.shape[0]
+    half = wproj.shape[1] // 2
+    row, me, group = lax.axis_index("dp"), lax.axis_index("tensor"), lax.axis_index("groups")
+    core, side = me % 2, me // 2
+    mate, across = side * 2 + 1 - core, (1 - side) * 2 + core
+    diag = (1 - side) * 2 + 1 - core
+
+    load_x = pltpu.make_async_copy(patches_hbm, patches, load_sem.at[0])
+    load_p = pltpu.make_async_copy(wproj_hbm, wproj.at[me], load_sem.at[1])
+    load_w = pltpu.make_async_copy(wqkv_hbm, wqkv, load_sem.at[2])
+    load_x.start()
+    load_p.start()
+    load_w.start()
+
+    barrier = pltpu.get_barrier_semaphore()
+    for k in range(1, nt):
+        pl.semaphore_signal(barrier, inc=1, device_id={"tensor": (me + k) % nt}, device_id_type=MESH)
+    for k in range(1, n):
+        pl.semaphore_signal(barrier, inc=1, device_id={"dp": (row + k) % n}, device_id_type=MESH)
+    pl.semaphore_signal(barrier, inc=1, device_id={"groups": 1 - group}, device_id_type=MESH)
+    pl.semaphore_wait(barrier, nt - 1 + n - 1 + 1)
+
+    def remote(source, target_ref, send, recv, device):
+        return pltpu.make_async_remote_copy(
+            source, target_ref, send, recv, device_id=device, device_id_type=MESH)
+
+    mine = pl.ds(pl.multiple_of(group * half, half), half)
+    other = pl.ds(pl.multiple_of((1 - group) * half, half), half)
+    proj_mate = remote(wproj.at[me], wproj.at[me], pm_send, p_recv.at[0], {"tensor": mate})
+    proj_across = remote(wproj.at[me, mine], wproj.at[me, mine], pa_send, p_recv.at[1], {"tensor": across})
+    proj_peer = remote(wproj.at[across, mine], wproj.at[across, mine], py_send, p_recv.at[2], {"groups": 1 - group})
+    proj_diag = [
+        remote(wproj.at[across, mine], wproj.at[across, mine], pd_send.at[0], pd_recv.at[0], {"tensor": mate}),
+        remote(wproj.at[across, other], wproj.at[across, other], pd_send.at[1], pd_recv.at[1], {"tensor": mate}),
+    ]
+    load_p.wait()
+    proj_across.start()
+    proj_mate.start()
+
+    live = grids[0, 0] * grids[0, 1]
+    dest_row = dest[...].astype(jnp.float32)
+
+    def shards(value):
+        total = jnp.zeros_like(value)
+        for s in range(1, n):
+            total += jnp.where(value >= float(s * seq_rows), 1.0, 0.0)
+        return total
+
+    square = (merged, merged)
+    first_at = lax.broadcasted_iota(jnp.int32, square, 0)
+    second_at = lax.broadcasted_iota(jnp.int32, square, 1)
+    dest_col = jnp.sum(jnp.where(first_at == second_at, dest_row, 0.0), axis=1, keepdims=True)
+    shard_row, shard_col = shards(dest_row), shards(dest_col)
+    rank_col = jnp.sum(
+        jnp.where((shard_row == shard_col) & (second_at < first_at), 1.0, 0.0), axis=1, keepdims=True)
+    live_col = lax.broadcasted_iota(jnp.int32, (merged, 1), 0) * 4 < live
+    lanes = 128
+    code_col = jnp.where(live_col, shard_col * lanes + rank_col, -1.0)
+    lane_at = lax.broadcasted_iota(jnp.int32, (merged, n * lanes), 1).astype(jnp.float32)
+    local_col = dest_col - shard_col * seq_rows
+    table = jnp.sum(jnp.where(lane_at == code_col, local_col + 1.0, 0.0), axis=0, keepdims=True) - 1.0
+    for s in range(n):
+        rows_tbl[s] = jnp.broadcast_to(table[:, s * lanes:(s + 1) * lanes], (8, lanes)).astype(jnp.int32)
+    arrived[row] = rows_tbl[row]
+
+    def send_table(k):
+        to = (row + k) % n
+        return remote(rows_tbl.at[to], arrived.at[row], tbl_send.at[k], tbl_recv.at[row], {"dp": to})
+
+    for k in range(1, n):
+        send_table(k).start()
+
+    wide = (merged, rows)
+    at_row = lax.broadcasted_iota(jnp.int32, wide, 0)
+    at_lane = lax.broadcasted_iota(jnp.int32, wide, 1)
+    dest_rep = jnp.sum(jnp.where(at_row == at_lane // 4, dest_col, 0.0), axis=0, keepdims=True)
+    shard_rep = shards(dest_rep)
+    rank_rep = jnp.sum(
+        jnp.where((shard_col == shard_rep) & (at_row < at_lane // 4), 1.0, 0.0), axis=0, keepdims=True)
+    piece = part // n
+    rank_i, shard_i = rank_rep.astype(jnp.int32), shard_rep.astype(jnp.int32)
+    place_i = lax.broadcasted_iota(jnp.int32, (1, rows), 1)
+    slot_i = rank_i // piece * block + place_i % 4 * part + shard_i * piece + rank_i % piece
+    target[...] = jnp.broadcast_to(jnp.where(place_i < live, slot_i, -1), target.shape)
+
+    load_x.wait()
+    load_w.wait()
+    lane80 = lax.broadcasted_iota(jnp.int32, (block, qs.shape[2]), 1)
+
+    def project(b, carry):
+        at = pl.ds(pl.multiple_of(b * block, block), block)
+        hit = jnp.where(
+            target[0:1, :] == lax.broadcasted_iota(jnp.int32, (block, rows), 0) + b * block, 1.0, 0.0)
+        valid = jnp.sum(hit, axis=1, keepdims=True)
+        raw = jnp.dot(hit.astype(jnp.bfloat16), patches[...], preferred_element_type=jnp.float32)
+
+        @pl.when(b == me)
+        def _():
+            own_rows[...] = raw.astype(jnp.bfloat16)
+
+        normed[...] = rms_scale(raw, gain[...]).astype(jnp.bfloat16)
+        for j, store in enumerate((qs, ks, vs)):
+            acc = jnp.dot(normed[...], wqkv[j], preferred_element_type=jnp.float32) + bqkv[j:j + 1, :]
+            extra = jnp.where(valid > 0.5, 0.0, -1e30) if j == 1 else jnp.ones((block, 1), jnp.float32)
+            fill = jnp.where(lane80 == HEAD_DIM, extra, 0.0).astype(jnp.bfloat16)
+            for h in range(heads):
+                store[h, at, :] = fill
+                store[h, at, 0:HEAD_DIM] = acc[:, h * HEAD_DIM:(h + 1) * HEAD_DIM].astype(jnp.bfloat16)
+        return carry
+
+    lax.fori_loop(0, n, project, 0)
+
+    proj_across.wait_recv()
+    proj_peer.start()
+    proj_diag[0].start()
+
+    scale = math.log2(math.e) / math.sqrt(HEAD_DIM)
+
+    def order(it):
+        return it % 2 * 2 + it // 2
+
+    def att_to(b):
+        return remote(att_out.at[b], att_in.at[me], att_send.at[b], att_recv.at[me], {"tensor": b})
+
+    def z_to(k):
+        to = (row + k) % n
+        return remote(slices.at[to], x_out.at[me, row], z_send.at[k], x_recv.at[me, row], {"dp": to})
+
+    def to_mate(i):
+        return remote(x_out.at[me, i], x_out.at[me, i], fm_send.at[i], x_recv.at[me, i], {"tensor": mate})
+
+    def to_across(i):
+        return remote(x_out.at[me, i], x_out.at[me, i], fa_send.at[i], x_recv.at[me, i], {"tensor": across})
+
+    def relay_mate(i):
+        return remote(
+            x_out.at[across, i], x_out.at[across, i], fx_send.at[i], x_recv.at[across, i], {"tensor": mate})
+
+    def landed(b, i):
+        return remote(x_out.at[b, i], x_out.at[b, i], fm_send.at[0], x_recv.at[b, i], {"tensor": mate})
+
+    def attend(it, carry):
+        @pl.when(it < n)
+        def _():
+            b = order(it)
+            at = pl.ds(pl.multiple_of(b * block, block), block)
+            for h in range(heads):
+                scores = lax.dot_general(
+                    qs[h, at, :], ks[h], (((1,), (1,)), ((), ())), preferred_element_type=jnp.float32)
+                peak = jnp.max(scores, axis=1, keepdims=True)
+                weights = jnp.exp2((scores - peak) * scale).astype(jnp.bfloat16)
+                mixed = jnp.dot(weights, vs[h], preferred_element_type=jnp.float32)
+                mixed = mixed * (1.0 / mixed[:, HEAD_DIM:HEAD_DIM + 1])
+                att_f32[:, h * HEAD_DIM:(h + 1) * HEAD_DIM] = mixed[:, 0:HEAD_DIM]
+            att_out[b] = att_f32[...].astype(jnp.bfloat16)
+
+            @pl.when(b != me)
+            def _():
+                att_to(b).start()
+
+            @pl.when(b == me)
+            def _():
+                att_in[me] = att_f32[...].astype(jnp.bfloat16)
+
+        @pl.when(it == 1)
+        def _():
+            proj_peer.wait_recv()
+            proj_diag[1].start()
+            proj_mate.wait_recv()
+            for copy in proj_diag:
+                copy.wait_recv()
+
+        @pl.when((it >= 1) & (order(lax.max(it, 1) - 1) == me))
+        def _():
+            for k in range(1, nt):
+                source = (me + k) % nt
+                remote(att_out.at[0], att_in.at[source], att_send.at[0], att_recv.at[source], {"tensor": mate}).wait_recv()
+            total = own_rows[...].astype(jnp.float32) + bproj[...]
+            for s in range(nt):
+                total += jnp.dot(att_in[s], wproj[s], preferred_element_type=jnp.float32)
+            ready = rms_scale(total, mgain[...]).astype(jnp.bfloat16)
+            for k in range(n):
+                slices[k] = ready[k * part:(k + 1) * part, :]
+            for k in range(1, n):
+                z_to(k).start()
+            x_out[me, row] = slices[row]
+            to_across(row).start()
+            to_mate(row).start()
+
+        return carry
+
+    lax.fori_loop(0, n + 1, attend, 0)
+
+    for k in range(1, n):
+        source = (row + n - k) % n
+        landed(me, source).wait_recv()
+        to_across(source).start()
+        to_mate(source).start()
+    for k in range(n):
+        source = (row + n - k) % n
+        landed(across, source).wait_recv()
+        relay_mate(source).start()
+    for k in range(n):
+        source = (row + n - k) % n
+        landed(mate, source).wait_recv()
+        landed(diag, source).wait_recv()
+    for k in range(1, n):
+        source = (row + n - k) % n
+        remote(rows_tbl.at[0], arrived.at[source], tbl_send.at[0], tbl_recv.at[source], {"dp": source}).wait_recv()
+
+    proj_mate.wait_send()
+    proj_across.wait_send()
+    proj_peer.wait_send()
+    for copy in proj_diag:
+        copy.wait_send()
+    for k in range(1, n):
+        send_table(k).wait_send()
+        z_to(k).wait_send()
+        att_to((me + k) % nt).wait_send()
+    for i in range(n):
+        to_mate(i).wait_send()
+        to_across(i).wait_send()
+        relay_mate(i).wait_send()
+
+
+def encode(patches, grids, dest, norm_gain, qkv_weight, qkv_bias, proj_weight, proj_bias, merge_gain, seq_rows):
+    n, nt = lax.axis_size("dp"), lax.axis_size("tensor")
+    rows, width = patches.shape
+    span = qkv_weight.shape[2]
+    heads = span // HEAD_DIM
+    block = rows // n
+    part = block // 4
+    any_space = pl.BlockSpec(memory_space=pl.ANY)
+    vmem = pl.BlockSpec(memory_space=pltpu.VMEM)
+    smem = pl.BlockSpec(memory_space=pltpu.SMEM)
+    dma = pltpu.SemaphoreType.DMA
+    bf16 = jnp.bfloat16
+    return pl.pallas_call(
+        functools.partial(encode_kernel, seq_rows),
+        out_shape=(
+            jax.ShapeDtypeStruct((n, n, part, width), bf16),
+            jax.ShapeDtypeStruct((n, 8, 128), jnp.int32),
+        ),
+        in_specs=[any_space, smem, vmem, vmem, any_space, vmem, any_space, vmem, vmem],
+        out_specs=(vmem, vmem),
+        scratch_shapes=[
+            pltpu.VMEM((rows, width), bf16),
+            pltpu.VMEM(qkv_weight.shape, bf16),
+            pltpu.VMEM((nt, span, width), bf16),
+            pltpu.VMEM((8, rows), jnp.int32),
+            pltpu.VMEM((block, width), bf16),
+            pltpu.VMEM((block, width), bf16),
+            pltpu.VMEM((heads, rows, 128), bf16),
+            pltpu.VMEM((heads, rows, 128), bf16),
+            pltpu.VMEM((heads, rows, 128), bf16),
+            pltpu.VMEM((block, span), jnp.float32),
+            pltpu.VMEM((n, block, span), bf16),
+            pltpu.VMEM((nt, block, span), bf16),
+            pltpu.VMEM((n, part, width), bf16),
+            pltpu.VMEM((n, 8, 128), jnp.int32),
+            dma((3,)), dma((n,)), dma((n,)), dma, dma, dma, dma((2,)), dma((3,)), dma((2,)),
+            dma((n,)), dma((nt,)), dma((n,)), dma((n,)), dma((n,)), dma((n,)), dma((nt, n)),
+        ],
+        compiler_params=pltpu.CompilerParams(
+            collective_id=2, has_side_effects=True, vmem_limit_bytes=60 * 1024 * 1024
+        ),
+    )(
+        patches, grids, dest, norm_gain.reshape(1, -1), qkv_weight, qkv_bias, proj_weight,
+        proj_bias.reshape(1, -1), merge_gain.reshape(1, -1),
+    )
+
+
+def merge_kernel(
+    lag, x, w1_hbm, bias, w2_hbm, out,
+    w1, w2, own, to_r, to_l, from_l, from_r, total, hidden, keep, give, from_mate, cross, from_across, ready, landed,
+    load_sem, r_send, r_recv, l_send, l_recv, mate_send, mate_recv, across_send, across_recv,
+    row_send, row_recv, end_send, end_recv,
+):
+    count, block, wide = own.shape
+    n, nt = x.shape[0], 4
+    pieces = count // n
+    quarter = keep.shape[3]
+    piece = ready.shape[3]
+    row, me = lax.axis_index("dp"), lax.axis_index("tensor")
+    core, side = me % 2, me // 2
+    mate, across = side * 2 + 1 - core, (1 - side) * 2 + core
+    left, right = lax.max(row - 1, 0), lax.min(row + 1, n - 1)
+    has_left, has_right = row > 0, row < n - 1
+
+    loads = [
+        pltpu.make_async_copy(a, b, load_sem.at[i]) for i, (a, b) in enumerate(((w1_hbm, w1), (w2_hbm, w2)))
+    ]
+    for load in loads:
+        load.start()
+
+    barrier = pltpu.get_barrier_semaphore()
+    for k in range(1, nt):
+        pl.semaphore_signal(barrier, inc=1, device_id={"tensor": (me + k) % nt}, device_id_type=MESH)
+    for k in range(1, n):
+        pl.semaphore_signal(barrier, inc=1, device_id={"dp": (row + k) % n}, device_id_type=MESH)
+    pl.semaphore_wait(barrier, nt - 1 + n - 1)
+
+    def remote(source, target, send, recv, device):
+        return pltpu.make_async_remote_copy(
+            source, target, send, recv, device_id=device, device_id_type=MESH)
+
+    def go_right(c):
+        return remote(to_r.at[c], from_l.at[c], r_send.at[c], r_recv.at[c], {"dp": right})
+
+    def go_left(c):
+        return remote(to_l.at[c], from_r.at[c], l_send.at[c], l_recv.at[c], {"dp": left})
+
+    def first(c):
+        columns = pl.ds(pl.multiple_of(c % pieces * wide, wide), wide)
+        partial = jnp.dot(
+            x[c // pieces].reshape(block, -1), w1[:, columns], preferred_element_type=jnp.float32)
+        own[c] = partial
+
+        @pl.when(row == 0)
+        def _():
+            to_r[c] = partial.astype(jnp.bfloat16)
+            go_right(c).start()
+
+        @pl.when(row == n - 1)
+        def _():
+            to_l[c] = partial.astype(jnp.bfloat16)
+            go_left(c).start()
+
+    def relay(stage, c):
+        @pl.when(row == stage)
+        def _():
+            go_right(c).wait_recv()
+            to_r[c] = (own[c] + from_l[c].astype(jnp.float32)).astype(jnp.bfloat16)
+            go_right(c).start()
+
+        @pl.when(row == n - 1 - stage)
+        def _():
+            go_left(c).wait_recv()
+            to_l[c] = (own[c] + from_r[c].astype(jnp.float32)).astype(jnp.bfloat16)
+            go_left(c).start()
+
+    def activate(c):
+        total[...] = own[c] + bias[c % pieces]
+
+        @pl.when(row == n - 1)
+        def _():
+            go_right(c).wait_recv()
+
+        @pl.when(row == 0)
+        def _():
+            go_left(c).wait_recv()
+
+        @pl.when(has_left)
+        def _():
+            total[...] += from_l[c].astype(jnp.float32)
+
+        @pl.when(has_right)
+        def _():
+            total[...] += from_r[c].astype(jnp.float32)
+
+        value = total[...]
+        hidden[c % pieces] = (0.5 * value * (1.0 + lax.erf(value * math.sqrt(0.5)))).astype(jnp.bfloat16)
+
+    def columns_of(s, c):
+        return pl.ds(pl.multiple_of((s * 2 + c) * quarter, quarter), quarter)
+
+    def to_mate(b, s):
+        return remote(give.at[b, s], from_mate.at[b, s], mate_send.at[b, s], mate_recv.at[b, s], {"tensor": mate})
+
+    def to_across(b):
+        return remote(cross.at[b], from_across.at[b], across_send.at[b], across_recv.at[b], {"tensor": across})
+
+    def to_row(b, k):
+        to = (row + k) % n
+        return remote(ready.at[b, to], landed.at[b, row], row_send.at[b, k], row_recv.at[b, row], {"dp": to})
+
+    def mine():
+        return pl.ds(pl.multiple_of(me * quarter, quarter), quarter)
+
+    def to_end(b, d):
+        return remote(
+            landed.at[b, d], out.at[:, b, :, mine()], end_send.at[b, d], end_recv.at[b, me], {"tensor": d})
+
+    def second(b):
+        def product(columns):
+            acc = jnp.dot(hidden[0], w2[0:wide, columns], preferred_element_type=jnp.float32)
+            for j in range(1, pieces):
+                acc += jnp.dot(hidden[j], w2[j * wide:(j + 1) * wide, columns], preferred_element_type=jnp.float32)
+            return acc
+
+        for s in (1 - side, side):
+            give[b, s] = product(columns_of(s, 1 - core)).astype(jnp.bfloat16)
+            to_mate(b, s).start()
+        for s in (1 - side, side):
+            keep[b, s] = product(columns_of(s, core))
+
+    def chip_sum(b):
+        to_mate(b, 1 - side).wait_recv()
+        cross[b] = (keep[b, 1 - side] + from_mate[b, 1 - side].astype(jnp.float32)).astype(jnp.bfloat16)
+        to_across(b).start()
+
+    def spread(b):
+        to_mate(b, side).wait_recv()
+        to_across(b).wait_recv()
+        value = keep[b, side] + from_mate[b, side].astype(jnp.float32) + from_across[b].astype(jnp.float32)
+        value = value.astype(jnp.bfloat16)
+        for i in range(n):
+            for s in range(n):
+                at = (i * n + s) * piece
+                ready[b, s, i] = value[at:at + piece, :]
+        for k in range(1, n):
+            to_row(b, k).start()
+        landed[b, row] = ready[b, row]
+
+    def deliver(b):
+        for k in range(n):
+            source = (row + n - k) % n
+            if k:
+                remote(
+                    ready.at[b, 0], landed.at[b, source], row_send.at[b, 0], row_recv.at[b, source], {"dp": left}
+                ).wait_recv()
+
+            @pl.when(source == me)
+            def _():
+                out[:, b, :, mine()] = landed[b, source]
+
+            @pl.when(source != me)
+            def _():
+                to_end(b, source).start()
+
+    loads[0].wait()
+    loads[1].wait()
+
+    ahead = (n - 1) * lag
+    after = ((0, second), (1, chip_sum), (3, spread), (5, deliver))
+
+    def step(s, carry):
+        @pl.when(s < count)
+        def _():
+            first(s)
+
+        for stage in range(1, n - 1):
+            @pl.when((s >= stage * lag) & (s < count + stage * lag))
+            def _():
+                relay(stage, s - stage * lag)
+
+        @pl.when((s >= ahead) & (s < count + ahead))
+        def _():
+            activate(s - ahead)
+
+        for offset, work in after:
+            at = s - ahead - offset + 1
+
+            @pl.when((at >= pieces) & (at <= count) & (lax.max(at, 0) % pieces == 0))
+            def _():
+                work(lax.max(at, pieces) // pieces - 1)
+
+        return carry
+
+    lax.fori_loop(0, count + ahead + 5, step, 0)
+
+    for b in range(n):
+        for k in range(1, nt):
+            source = (me + k) % nt
+            columns = pl.ds(pl.multiple_of(source * quarter, quarter), quarter)
+            remote(
+                landed.at[b, 0], out.at[:, b, :, columns], end_send.at[b, 0], end_recv.at[b, source], {"tensor": mate}
+            ).wait_recv()
+
+    def drain(c, carry):
+        @pl.when(has_right)
+        def _():
+            go_right(c).wait_send()
+
+        @pl.when(has_left)
+        def _():
+            go_left(c).wait_send()
+
+        return carry
+
+    lax.fori_loop(0, count, drain, 0)
+    for b in range(n):
+        for s in range(2):
+            to_mate(b, s).wait_send()
+        to_across(b).wait_send()
+        for k in range(1, n):
+            to_row(b, k).wait_send()
+            to_end(b, (me + k) % nt).wait_send()
+
+
+def merge(x, w1, bias, w2):
+    n, _, part, depth = x.shape
+    block = n * part
+    hidden, columns = w2.shape
+    wide = 256
+    pieces = hidden // wide
+    count = n * pieces
+    quarter = columns // 4
+    piece = part // n
+    any_space = pl.BlockSpec(memory_space=pl.ANY)
+    vmem = pl.BlockSpec(memory_space=pltpu.VMEM)
+    dma = pltpu.SemaphoreType.DMA
+    bf16, f32 = jnp.bfloat16, jnp.float32
+    stack = pltpu.VMEM((count, block, wide), bf16)
+    tiles = pltpu.VMEM((n, 2, block, quarter), bf16)
+    one = pltpu.VMEM((n, block, quarter), bf16)
+    moved = pltpu.VMEM((n, n, n, piece, quarter), bf16)
+    return pl.pallas_call(
+        functools.partial(merge_kernel, 2),
+        out_shape=jax.ShapeDtypeStruct((n, n, piece, columns), bf16),
+        in_specs=[vmem, any_space, vmem, any_space],
+        out_specs=vmem,
+        scratch_shapes=[
+            pltpu.VMEM(w1.shape, bf16),
+            pltpu.VMEM(w2.shape, bf16),
+            pltpu.VMEM((count, block, wide), f32),
+            stack, stack, stack, stack,
+            pltpu.VMEM((block, wide), f32),
+            pltpu.VMEM((pieces, block, wide), bf16),
+            pltpu.VMEM((n, 2, block, quarter), f32),
+            tiles, tiles, one, one, moved, moved,
+            dma((2,)), dma((count,)), dma((count,)), dma((count,)), dma((count,)),
+            dma((n, 2)), dma((n, 2)), dma((n,)), dma((n,)), dma((n, n)), dma((n, n)), dma((n, 4)), dma((n, 4)),
+        ],
+        compiler_params=pltpu.CompilerParams(
+            collective_id=3, has_side_effects=True, vmem_limit_bytes=62 * 1024 * 1024
+        ),
+    )(x, w1, bias.reshape(pieces, 1, wide), w2)
+
+
+def local_fast(
+    patches,
+    grids,
+    dest,
+    norm_gain,
+    qkv_weight,
+    qkv_bias,
+    proj_weight,
+    proj_bias,
+    merge_gain,
+    w_first,
+    b_first,
+    w_second,
+    b_second,
+    text_embed,
+):
+    seq_rows = text_embed.shape[0]
+    x, arrived = encode(
+        patches, grids, dest, norm_gain, qkv_weight, qkv_bias, proj_weight, proj_bias, merge_gain, seq_rows)
+    visual = merge(x, w_first, b_first, w_second)
+    capacity = x.shape[2]
+    visual = visual.reshape(-1, visual.shape[3])
+    arrived_rows = arrived[:, 0, :capacity].reshape(-1)
+    visual = (visual.astype(jnp.float32) + b_second).astype(jnp.bfloat16)
+    hit = jnp.arange(seq_rows, dtype=jnp.int32)[:, None] == arrived_rows[None, :]
+    placed = jnp.dot(hit.astype(jnp.bfloat16), visual, preferred_element_type=jnp.float32).astype(jnp.bfloat16)
+    return jnp.where(jnp.any(hit, axis=1)[:, None], placed, text_embed)
+
+
+def fits(patches, grids, dest, qkv_weight, w_first, w_second):
+    n, nt = lax.axis_size("dp"), lax.axis_size("tensor")
+    rows, width = patches.shape
+    return (
+        n == nt == 4
+        and lax.axis_size("groups") == 2
+        and grids.shape[0] == 1
+        and rows == PATCHES
+        and dest.shape[1] == MERGED
+        and w_first.shape[0] == width
+        and w_second.shape[0] % 256 == 0
+        and w_second.shape[1] % 512 == 0
+        and qkv_weight.shape[2] % 32 == 0
+    )
+
+
+def chosen(*args):
+    run = local_fast if fits(args[0], args[1], args[2], args[4], args[9], args[11]) else local
+    return run(*args)
+
+
 def solution(mesh):
     in_specs = (
         P(("groups", "dp"), None),
@@ -543,4 +1133,4 @@
         P(("groups", "dp"), "tensor"),
     )
     out_specs = P(("groups", "dp"), "tensor")
-    return jax.shard_map(local, mesh=mesh, in_specs=in_specs, out_specs=out_specs, check_vma=False)
+    return jax.shard_map(chosen, mesh=mesh, in_specs=in_specs, out_specs=out_specs, check_vma=False)

time: 289 us -> 179 us (0.62)
  waiting for transfers between devices: 55.1 us -> 0 us
  matrix products: 26 us -> 3 us
  blocking collectives: 20.5 us -> 0 us
  Pallas kernels: 149 us -> 165 us
  between operations: 14.9 us -> 0.05 us
  other arithmetic: 7.38 us -> 0.15 us
  local copies, waits for them, and re-layouts: 12.5 us -> 8.51 us
  starting transfers between devices: 3.32 us -> 0 us
    reduce_scatter x1 -> x0, waiting for transfers between devices: 36.5 us -> none  [local(): lax.psum_scatter(partial_value, 'tensor', scatter_dimension=0, tiled=True)]
    all_to_all x1 -> x0, blocking collectives: 20.5 us -> none  [local(): lax.all_to_all(merged_in.reshape(part // 4, dp_count, 4 * width // dp_cou...]
    pallas_call x2, Pallas kernels: 149 us -> 165 us  [the longest x1 109 us: merge(): pl.pallas_call(functools.partial(merge_kernel, 2), out_shape=jax.ShapeDty...]
    all_gather x1 -> x0, waiting for transfers between devices: 15.6 us -> none  [local(): received = lax.all_gather(sliced, 'tensor', axis=1, tiled=False)]
    dot_general x4 -> x1, matrix products: 15.1 us -> 3 us  [local_fast(): jnp.dot(hit.astype(jnp.bfloat16), visual, preferred_element_type=jnp.floa...]
    sub x1 -> x0, matrix products: 10.9 us -> none  [attention(): exponent = jnp.exp(scores - peak_score)]
    reduce_sum x3 -> x0, other arithmetic: 4.19 us -> none  [the longest x2 4.01 us: rms_scale(): jnp.mean(values * values, axis=-1, keepdims=True) + 1e-06]
    all_gather x1 -> x0, local copies, waits for them, and re-layouts: 3.52 us -> none  [local(): received = lax.all_gather(sliced, 'tensor', axis=1, tiled=False)]
  transfers between devices with their start and end apart: 3 -> 0, of which waited for: 3 -> 0; matrix products, arithmetic and copies ran while one was open for 1% -> 0% of each run, Pallas kernels for 0% -> 0%
where the time goes in v1:
time: 179 us; the launch traced here: 177 us
  Pallas kernels  165 us (92%)
  local copies, waits for them, and re-layouts  8.51 us (5%)
  matrix products  3 us (2%)
    pallas_call x1, Pallas kernels, merge(): pl.pallas_call(functools.partial(merge_kernel, 2), out_shape=jax.ShapeDty...  109 us
    pallas_call x1, Pallas kernels, encode(): pl.pallas_call(functools.partial(encode_kernel, seq_rows), out_shape=(jax...  56.5 us
    unnamed x13, local copies, waits for them, and re-layouts  5.31 us

profile of v1, /device:TPU:1, one launch (start us, length us, event | category | flops | bytes accessed | tf_op | source)
XLA Modules:
  0.0 177.1 jit_solution(7548412692244279613)
XLA Ops:
  0.0 0.0 copy-start
  0.0 0.0 copy-start.1
  0.0 0.0 copy-start.2
  0.0 5.3 %copy.16.wqkv_hbm = bf16[3,1280,320]{2,1,0:T(8,128)(2,1)} copy(bf16[3,1280,320]{1,2,0:T(8,128)(2,1)} %param.18) | data formatting | bytes 4915200 | tf_op args[4]
  5.3 0.0 copy-done
  5.3 0.6 reshape.18.gain
  5.9 0.0 copy-done.1
  5.9 0.6 reshape.19.bproj
  6.5 0.0 copy-done.2
  6.5 0.6 reshape.20.mgain
  7.1 0.0 copy-start.3
  7.1 56.5 %shard_map.136 = (bf16[4,4,64,1280]{3,2,1,0:T(8,128)(2,1)}, s32[4,8,128]{2,1,0:T(8,128)}) custom-call(bf16[1024,1280]{1,0:T(8,128)(2,1)} %patches_hbm.1, s32[1,2]{1,0:T(1,128)} %grids.1, s32[1,256]{1,0:T(1,128)} %dest.1, f32[1,1280]{1,0:T(1,128)} %reshape.18.gain, bf16[3,1280,320]{2,1,0:T(8,128)(2,1)} %copy.16.wqkv_hbm, f32[3,320]{1,0:T(4,128)} %bqkv.1, ...), custom_call_target="tpu_custom_call" | custom-call | tf_op jit(solution)/shard_map/pallas_call | solution.py:775
  63.6 0.7 slice_reduce_fusion
  64.4 0.1 eq.16
  64.5 0.2 fusion.4
  64.6 0.0 copy-done.3
  64.6 0.6 reshape.21.bias
  65.2 0.0 copy-start.4
  65.2 0.0 copy-start.5
  65.2 108.9 %shard_map.137 = bf16[4,4,16,2048]{3,2,1,0:T(8,128)(2,1)} custom-call(bf16[4,4,64,1280]{3,2,1,0:T(8,128)(2,1)} %get-tuple-element.8.x, bf16[1280,1280]{1,0:T(8,128)(2,1)} %w1_hbm.1, f32[5,1,256]{2,1,0:T(1,128)} %reshape.21.bias, bf16[1280,2048]{1,0:T(8,128)(2,1)} %w2_hbm.1), custom_call_target="tpu_custom_call" | custom-call | tf_op jit(solution)/shard_map/pallas_call | solution.py:1045
  174.1 0.0 copy-done.4
  174.1 0.0 copy-done.5
  174.1 3.0 %fusion = bf16[384,2048]{1,0:T(8,128)(2,1)} fusion(bf16[384,2048]{1,0:T(8,128)(2,1)S(1)} %copy-done.4, pred[384]{0:T(512)(128)(4,1)S(1)} %fusion.4, bf16[256,2048]{1,0:T(8,128)(2,1)} %bitcast.2, f32[2048]{0:T(1024)S(1)} %copy-done.5, s32[256]{0:T(256)S(1)} %eq.16), kind=kOutput, calls=%fused_computation.1 | convolution fusion | flops 405897216 | bytes 4203904 | tf_op jit(solution)/shard_map/dot_general | solution.py:1093
Async XLA Ops:
  0.0 5.3 %copy-start = (f32[1280]{0:T(1024)S(1)}, f32[1280]{0:T(1024)}, u32[]{:S(2)}) copy-start(f32[1280]{0:T(1024)} %param.17) | copy-start | bytes 15364
  0.0 5.9 %copy-start.1 = (f32[1280]{0:T(1024)S(1)}, f32[1280]{0:T(1024)}, u32[]{:S(2)}) copy-start(f32[1280]{0:T(1024)} %param.21) | copy-start | bytes 15364
  0.0 6.5 %copy-start.2 = (f32[1280]{0:T(1024)S(1)}, f32[1280]{0:T(1024)}, u32[]{:S(2)}) copy-start(f32[1280]{0:T(1024)} %param.22) | copy-start | bytes 15364
  7.1 57.5 %copy-start.3 = (f32[1280]{0:T(1024)S(1)}, f32[1280]{0:T(1024)}, u32[]{:S(2)}) copy-start(f32[1280]{0:T(1024)} %param.24) | copy-start | bytes 15364
  65.2 108.9 %copy-start.4 = (bf16[384,2048]{1,0:T(8,128)(2,1)S(1)}, bf16[384,2048]{1,0:T(8,128)(2,1)}, u32[]{:S(2)}) copy-start(bf16[384,2048]{1,0:T(8,128)(2,1)} %param.27) | copy-start | bytes 4718596
  65.2 108.9 %copy-start.5 = (f32[2048]{0:T(1024)S(1)}, f32[2048]{0:T(1024)}, u32[]{:S(2)}) copy-start(f32[2048]{0:T(1024)} %param.26) | copy-start | bytes 24580

commit v2 on v0

--- a/solution.py
+++ b/solution.py
@@ -525,6 +525,647 @@
     return jnp.where(jnp.any(hit, axis=1)[:, None], placed, text_embed)
 
 
+def fused_kernel(
+    seq_rows, lags,
+    patches_hbm, grids, dest, gain, wqkv_hbm, bqkv, wproj_hbm, bproj, mgain, w1_hbm, bias, w2_hbm,
+    out, arrived,
+    patches, wqkv, bpad, wproj, target, normed, raws, qs, ks, vs, att_f32, att_out, att_in, slices, rows_tbl, x,
+    w1, w2, own, to_r, to_l, from_l, from_r, hidden, keep, give, from_mate, cross, from_across, ready, landed,
+    load_sem, head_sem, tbl_send, tbl_recv, pm_send, pm_recv, pa_send, pa_recv, py_send, py_recv, pd_send, pd_recv,
+    att_send, att_recv, z_send, fm_send, fa_send, x_recv,
+    r_send, r_recv, l_send, l_recv, mate_send, mate_recv, across_send, across_recv,
+    row_send, row_recv, end_send, end_recv,
+):
+    n, sides, _, few, width = x.shape
+    nt = 2 * sides
+    rows = patches.shape[0]
+    block = rows // n
+    half = block // sides
+    merged = dest.shape[1]
+    heads = qs.shape[0]
+    lanes = qs.shape[2]
+    count, _, wide = own.shape
+    steps = count // n
+    pieces = steps // sides
+    quarter = keep.shape[2]
+    piece = ready.shape[3]
+    row, me, group = lax.axis_index("dp"), lax.axis_index("tensor"), lax.axis_index("groups")
+    core, side = me % 2, me // 2
+    mate, across = side * 2 + 1 - core, (1 - side) * 2 + core
+    left, right = lax.max(row - 1, 0), lax.min(row + 1, n - 1)
+    has_left, has_right = row > 0, row < n - 1
+    bf16, f32 = jnp.bfloat16, jnp.float32
+
+    load_x = pltpu.make_async_copy(patches_hbm, patches, load_sem.at[0])
+    load_p = pltpu.make_async_copy(wproj_hbm, wproj.at[me], load_sem.at[1])
+    load_1 = pltpu.make_async_copy(w1_hbm, w1, load_sem.at[2])
+    load_2 = pltpu.make_async_copy(w2_hbm, w2, load_sem.at[3])
+    load_w = [
+        pltpu.make_async_copy(
+            wqkv_hbm.at[j, h * HEAD_DIM:(h + 1) * HEAD_DIM], wqkv.at[j, h * lanes:h * lanes + HEAD_DIM],
+            head_sem.at[j, h])
+        for j in range(3) for h in range(heads)
+    ]
+    load_p.start()
+    load_x.start()
+    for load in load_w:
+        load.start()
+
+    barrier = pltpu.get_barrier_semaphore()
+    for k in range(1, nt):
+        pl.semaphore_signal(barrier, inc=1, device_id={"tensor": (me + k) % nt}, device_id_type=MESH)
+    for k in range(1, n):
+        pl.semaphore_signal(barrier, inc=1, device_id={"dp": (row + k) % n}, device_id_type=MESH)
+    pl.semaphore_signal(barrier, inc=1, device_id={"groups": 1 - group}, device_id_type=MESH)
+    pl.semaphore_wait(barrier, nt - 1 + n - 1 + 1)
+
+    def remote(source, to, send, recv, device):
+        return pltpu.make_async_remote_copy(source, to, send, recv, device_id=device, device_id_type=MESH)
+
+    span = wproj.shape[1] // 4
+
+    def strip(g, a):
+        return pl.ds(pl.multiple_of((g * 2 + a) * span, span), span)
+
+    def same(ref, send, recv, device):
+        return remote(ref, ref, send, recv, device)
+
+    proj_mate = same(wproj.at[me], pm_send, pm_recv, {"tensor": mate})
+    proj_across = [
+        same(wproj.at[me, strip(group, a)], pa_send.at[a], pa_recv.at[a], {"tensor": across}) for a in range(2)]
+    proj_got = [
+        same(wproj.at[across, strip(group, a)], pa_send.at[a], pa_recv.at[a], {"tensor": across}) for a in range(2)]
+    proj_peer = [
+        same(wproj.at[across, strip(group, a)], py_send.at[a], py_recv.at[a], {"groups": 1 - group})
+        for a in range(2)]
+    proj_peer_got = [
+        same(wproj.at[across, strip(1 - group, a)], py_send.at[a], py_recv.at[a], {"groups": 1 - group})
+        for a in range(2)]
+
+    def proj_diag(g, a, at):
+        return same(wproj.at[across, strip(g, a)], pd_send.at[at, a], pd_recv.at[at, a], {"tensor": mate})
+
+    load_p.wait()
+    for copy in proj_across:
+        copy.start()
+    proj_mate.start()
+
+    live = grids[0, 0] * grids[0, 1]
+    dest_row = dest[...].astype(f32)
+
+    def shards(value):
+        total = jnp.zeros_like(value)
+        for s in range(1, n):
+            total += jnp.where(value >= float(s * seq_rows), 1.0, 0.0)
+        return total
+
+    square = (merged, merged)
+    first_at = lax.broadcasted_iota(jnp.int32, square, 0)
+    second_at = lax.broadcasted_iota(jnp.int32, square, 1)
+    dest_col = jnp.sum(jnp.where(first_at == second_at, dest_row, 0.0), axis=1, keepdims=True)
+    shard_row, shard_col = shards(dest_row), shards(dest_col)
+    rank_col = jnp.sum(
+        jnp.where((shard_row == shard_col) & (second_at < first_at), 1.0, 0.0), axis=1, keepdims=True)
+    live_col = lax.broadcasted_iota(jnp.int32, (merged, 1), 0) * 4 < live
+    code_col = jnp.where(live_col, shard_col * lanes + rank_col, -1.0)
+    lane_at = lax.broadcasted_iota(jnp.int32, (merged, n * lanes), 1).astype(f32)
+    local_col = dest_col - shard_col * seq_rows
+    table = jnp.sum(jnp.where(lane_at == code_col, local_col + 1.0, 0.0), axis=0, keepdims=True) - 1.0
+    for s in range(n):
+        rows_tbl[s] = jnp.broadcast_to(table[:, s * lanes:(s + 1) * lanes], (8, lanes)).astype(jnp.int32)
+    arrived[row] = rows_tbl[row]
+
+    def send_table(k):
+        to = (row + k) % n
+        return remote(rows_tbl.at[to], arrived.at[row], tbl_send.at[k], tbl_recv.at[row], {"dp": to})
+
+    for k in range(1, n):
+        send_table(k).start()
+
+    tall = (merged, rows)
+    at_row = lax.broadcasted_iota(jnp.int32, tall, 0)
+    at_lane = lax.broadcasted_iota(jnp.int32, tall, 1)
+    dest_rep = jnp.sum(jnp.where(at_row == at_lane // 4, dest_col, 0.0), axis=0, keepdims=True)
+    shard_rep = shards(dest_rep)
+    rank_rep = jnp.sum(
+        jnp.where((shard_col == shard_rep) & (at_row < at_lane // 4), 1.0, 0.0), axis=0, keepdims=True)
+    rank_i, shard_i = rank_rep.astype(jnp.int32), shard_rep.astype(jnp.int32)
+    place_i = lax.broadcasted_iota(jnp.int32, (1, rows), 1)
+    slot_i = (
+        rank_i // piece * block + shard_i // 2 * half + place_i % 4 * few + shard_i % 2 * piece + rank_i % piece)
+    target[...] = jnp.broadcast_to(jnp.where(place_i < live, slot_i, -1), target.shape)
+
+    ones_at = lax.broadcasted_iota(jnp.int32, (1, lanes), 1) == HEAD_DIM
+    for j in range(3):
+        for h in range(heads):
+            bpad[j:j + 1, h * lanes:(h + 1) * lanes] = jnp.where(ones_at, 0.0 if j == 1 else 1.0, 0.0)
+            bpad[j:j + 1, h * lanes:h * lanes + HEAD_DIM] = bqkv[j:j + 1, h * HEAD_DIM:(h + 1) * HEAD_DIM]
+            wqkv[j, h * lanes + HEAD_DIM:(h + 1) * lanes, :] = jnp.zeros((lanes - HEAD_DIM, width), bf16)
+
+    load_x.wait()
+    for load in load_w:
+        load.wait()
+    load_1.start()
+    load_2.start()
+
+    mask_at = lax.broadcasted_iota(jnp.int32, (block, lanes), 1) == HEAD_DIM
+
+    def project(b, carry):
+        @pl.when(b == 2)
+        def _():
+            proj_got[0].wait_recv()
+            proj_peer[0].start()
+            proj_diag(group, 0, 0).start()
+
+        at = pl.ds(pl.multiple_of(b * block, block), block)
+        hit = jnp.where(
+            target[0:1, :] == lax.broadcasted_iota(jnp.int32, (block, rows), 0) + b * block, 1.0, 0.0)
+        valid = jnp.sum(hit, axis=1, keepdims=True)
+        raw = jnp.dot(hit.astype(bf16), patches[...], preferred_element_type=f32)
+        for s in range(sides):
+            raws[b, s] = raw[s * half:(s + 1) * half, :].astype(bf16)
+        normed[...] = rms_scale(raw, gain[...].reshape(1, width)).astype(bf16)
+        for j, store in enumerate((qs, ks, vs)):
+            acc = lax.dot_general(
+                normed[...], wqkv[j], (((1,), (1,)), ((), ())), preferred_element_type=f32) + bpad[j:j + 1, :]
+            for h in range(heads):
+                value = acc[:, h * lanes:(h + 1) * lanes]
+                if j == 1:
+                    value = jnp.where(mask_at, jnp.where(valid > 0.5, 0.0, -1e30), value)
+                store[h, at, :] = value.astype(bf16)
+        return carry
+
+    lax.fori_loop(0, n, project, 0)
+
+    proj_got[1].wait_recv()
+    proj_peer[1].start()
+    proj_diag(group, 1, 0).start()
+
+    scale = math.log2(math.e) / math.sqrt(HEAD_DIM)
+
+    def att_to(b, s):
+        return remote(
+            att_out.at[b, s], att_in.at[b // 2, me], att_send.at[b, s], att_recv.at[b // 2, me],
+            {"tensor": s * 2 + b % 2})
+
+    def att_got(b, source):
+        return remote(
+            att_out.at[b, 0], att_in.at[b // 2, source], att_send.at[b, 0], att_recv.at[b // 2, source],
+            {"tensor": mate})
+
+    def z_to(b, k):
+        to = (row + k) % n
+        return remote(
+            slices.at[b // 2, to], x.at[b, side, row], z_send.at[b // 2, k], x_recv.at[b, side, row], {"dp": to})
+
+    def to_mate_x(b, s, i):
+        return same(x.at[b, s, i], fm_send.at[b // 2, s, i], x_recv.at[b, s, i], {"tensor": mate})
+
+    def to_across_x(b, i):
+        return same(x.at[b, side, i], fa_send.at[b // 2, i], x_recv.at[b, side, i], {"tensor": across})
+
+    def x_got(b, s, i):
+        return same(x.at[b, s, i], fm_send.at[b // 2, s, i], x_recv.at[b, s, i], {"tensor": mate})
+
+    def attend(it, carry):
+        @pl.when(it < n)
+        def _():
+            b = lax.min(it, n - 1)
+            at = pl.ds(pl.multiple_of(b * block, block), block)
+            for h in range(heads):
+                scores = lax.dot_general(
+                    qs[h, at, :], ks[h], (((1,), (1,)), ((), ())), preferred_element_type=f32)
+                peak = jnp.max(scores, axis=1, keepdims=True)
+                weights = jnp.exp2((scores - peak) * scale).astype(bf16)
+                mixed = jnp.dot(weights, vs[h], preferred_element_type=f32)
+                mixed = mixed * (1.0 / mixed[:, HEAD_DIM:HEAD_DIM + 1])
+                att_f32[:, h * HEAD_DIM:(h + 1) * HEAD_DIM] = mixed[:, 0:HEAD_DIM]
+            for s in range(sides):
+                att_out[b, s] = att_f32[s * half:(s + 1) * half, :].astype(bf16)
+                owner = s * 2 + b % 2
+
+                @pl.when(owner != me)
+                def _():
+                    att_to(b, s).start()
+
+                @pl.when(owner == me)
+                def _():
+                    att_in[b // 2, me] = att_out[b, s]
+
+        @pl.when(it == 1)
+        def _():
+            proj_mate.wait_recv()
+            for a in range(2):
+                proj_peer_got[a].wait_recv()
+                proj_diag(1 - group, a, 1).start()
+            for a in range(2):
+                proj_diag(group, a, 0).wait_recv()
+                proj_diag(1 - group, a, 1).wait_recv()
+
+        last = lax.max(it, 1) - 1
+
+        @pl.when((it >= 1) & (last % 2 == core))
+        def _():
+            for k in range(1, nt):
+                att_got(last, (me + k) % nt).wait_recv()
+            total = raws[last, side].astype(f32) + bproj[...].reshape(1, width)
+            for t in range(nt):
+                total += jnp.dot(att_in[last // 2, t], wproj[t], preferred_element_type=f32)
+            done = rms_scale(total, mgain[...].reshape(1, width)).astype(bf16)
+            for k in range(n):
+                slices[last // 2, k] = done[k * few:(k + 1) * few, :]
+            for k in range(n - 1, 0, -1):
+                z_to(last, k).start()
+            x[last, side, row] = slices[last // 2, row]
+            to_across_x(last, row).start()
+            to_mate_x(last, side, row).start()
+
+        return carry
+
+    lax.fori_loop(0, n + 1, attend, 0)
+
+    def forward(b):
+        for k in range(1, n):
+            source = (row + n - k) % n
+            x_got(b, side, source).wait_recv()
+            to_across_x(b, source).start()
+            to_mate_x(b, side, source).start()
+
+    def forward_across(b):
+        for k in range(n):
+            source = (row + n - k) % n
+            x_got(b, 1 - side, source).wait_recv()
+            to_mate_x(b, 1 - side, source).start()
+
+    def await_x(b):
+        @pl.when(b % 2 != core)
+        def _():
+            for s in range(sides):
+                for i in range(n):
+                    x_got(b, s, i).wait_recv()
+
+    def go_right(c):
+        return remote(to_r.at[c], from_l.at[c], r_send.at[c], r_recv.at[c], {"dp": right})
+
+    def go_left(c):
+        return remote(to_l.at[c], from_r.at[c], l_send.at[c], l_recv.at[c], {"dp": left})
+
+    def first(c):
+        b, j = c // steps, c % steps // sides
+        columns = pl.ds(pl.multiple_of(j * wide, wide), wide)
+        partial = jnp.dot(x[b].reshape(block, width), w1[:, columns], preferred_element_type=f32)
+        for s in range(sides):
+            own[c + s] = partial[s * half:(s + 1) * half, :]
+
+            @pl.when(row == 0)
+            def _():
+                to_r[c + s] = partial[s * half:(s + 1) * half, :].astype(bf16)
+                go_right(c + s).start()
+
+            @pl.when(row == n - 1)
+            def _():
+                to_l[c + s] = partial[s * half:(s + 1) * half, :].astype(bf16)
+                go_left(c + s).start()
+
+    def relay(stage, c):
+        @pl.when(row == stage)
+        def _():
+            go_right(c).wait_recv()
+            to_r[c] = (own[c] + from_l[c].astype(f32)).astype(bf16)
+            go_right(c).start()
+
+        @pl.when(row == n - 1 - stage)
+        def _():
+            go_left(c).wait_recv()
+            to_l[c] = (own[c] + from_r[c].astype(f32)).astype(bf16)
+            go_left(c).start()
+
+    def activate(c):
+        j = c % steps // sides
+
+        @pl.when(row == n - 1)
+        def _():
+            go_right(c).wait_recv()
+
+        @pl.when(row == 0)
+        def _():
+            go_left(c).wait_recv()
+
+        @pl.when(has_left)
+        def _():
+            own[c] += from_l[c].astype(f32)
+
+        @pl.when(has_right)
+        def _():
+            own[c] += from_r[c].astype(f32)
+
+        value = own[c] + bias[j]
+        at = pl.ds(pl.multiple_of(c % sides * half, half), half)
+        hidden[j, at, :] = (0.5 * value * (1.0 + lax.erf(value * math.sqrt(0.5)))).astype(bf16)
+
+    def columns_of(s, c):
+        return pl.ds(pl.multiple_of((s * 2 + c) * quarter, quarter), quarter)
+
+    def to_mate(b, s):
+        return remote(give.at[b, s], from_mate.at[b, s], mate_send.at[b, s], mate_recv.at[b, s], {"tensor": mate})
+
+    def to_across(b):
+        return remote(cross.at[b], from_across.at[b], across_send.at[b], across_recv.at[b], {"tensor": across})
+
+    def to_row(b, k):
+        to = (row + k) % n
+        return remote(ready.at[b, to], landed.at[b, row], row_send.at[b, k], row_recv.at[b, row], {"dp": to})
+
+    def quarter_of(t):
+        return pl.ds(pl.multiple_of(t * quarter, quarter), quarter)
+
+    def to_end(b, d):
+        return remote(
+            landed.at[b, d], out.at[:, b, :, quarter_of(me)], end_send.at[b, d], end_recv.at[b, me], {"tensor": d})
+
+    def second(b):
+        def product(columns):
+            acc = jnp.dot(hidden[0], w2[0:wide, columns], preferred_element_type=f32)
+            for j in range(1, pieces):
+                acc += jnp.dot(hidden[j], w2[j * wide:(j + 1) * wide, columns], preferred_element_type=f32)
+            return acc
+
+        for s in (1 - side, side):
+            give[b, s] = product(columns_of(s, 1 - core)).astype(bf16)
+            to_mate(b, s).start()
+        for s in (1 - side, side):
+            keep[s] = product(columns_of(s, core))
+
+    def chip_sum(b):
+        to_mate(b, 1 - side).wait_recv()
+        cross[b] = (keep[1 - side] + from_mate[b, 1 - side].astype(f32)).astype(bf16)
+        to_across(b).start()
+
+    def spread(b):
+        to_mate(b, side).wait_recv()
+        to_across(b).wait_recv()
+        value = keep[side] + from_mate[b, side].astype(f32) + from_across[b].astype(f32)
+        value = value.astype(bf16)
+        for s in range(n):
+            for i in range(n):
+                at = s // 2 * half + i * few + s % 2 * piece
+                ready[b, s, i] = value[at:at + piece, :]
+        for k in range(n - 1, 0, -1):
+            to_row(b, k).start()
+        landed[b, row] = ready[b, row]
+
+    def deliver(b):
+        for k in range(n):
+            source = (row + n - k) % n
+            if k:
+                remote(
+                    ready.at[b, 0], landed.at[b, source], row_send.at[b, 0], row_recv.at[b, source], {"dp": left}
+                ).wait_recv()
+
+            @pl.when(source == me)
+            def _():
+                out[:, b, :, quarter_of(me)] = landed[b, source]
+
+            @pl.when(source != me)
+            def _():
+                to_end(b, source).start()
+
+    lead, hop, fill, offsets = lags
+
+    @pl.when(core == 0)
+    def _():
+        forward(0)
+        forward_across(0)
+
+    @pl.when(core == 1)
+    def _():
+        forward(1)
+
+    load_1.wait()
+    load_2.wait()
+    after = tuple(zip(offsets, (second, chip_sum, spread, deliver)))
+
+    def step(u, carry):
+        @pl.when((u < count) & (u % sides == 0))
+        def _():
+            @pl.when(u % steps == 0)
+            def _():
+                await_x(u // steps)
+
+            first(u)
+
+        @pl.when((u == 1) & (core == 1))
+        def _():
+            forward_across(1)
+
+        @pl.when(u == 3)
+        def _():
+            forward(2 + core)
+
+        @pl.when(u == 5)
+        def _():
+            forward_across(2 + core)
+
+        for stage in range(1, n - 1):
+            late = lead + (stage - 1) * hop
+
+            @pl.when((u >= late) & (u < count + late))
+            def _():
+                relay(stage, u - late)
+
+        @pl.when((u >= lead + fill) & (u < count + lead + fill))
+        def _():
+            activate(u - lead - fill)
+
+        for offset, work in after:
+            late = lead + fill + offset + steps - 1
+
+            @pl.when((u >= late) & (u < count + late) & (lax.max(u - late, 0) % steps == 0))
+            def _():
+                work((u - late) // steps)
+
+        return carry
+
+    lax.fori_loop(0, count + lead + fill + offsets[-1], step, 0)
+
+    for b in range(n):
+        for k in range(1, nt):
+            source = (me + k) % nt
+            remote(
+                landed.at[b, 0], out.at[:, b, :, quarter_of(source)], end_send.at[b, 0], end_recv.at[b, source],
+                {"tensor": mate},
+            ).wait_recv()
+    for k in range(1, n):
+        source = (row + n - k) % n
+        remote(rows_tbl.at[0], arrived.at[source], tbl_send.at[0], tbl_recv.at[source], {"dp": source}).wait_recv()
+
+    def drain(c, carry):
+        @pl.when(has_right)
+        def _():
+            go_right(c).wait_send()
+
+        @pl.when(has_left)
+        def _():
+            go_left(c).wait_send()
+
+        return carry
+
+    lax.fori_loop(0, count, drain, 0)
+    proj_mate.wait_send()
+    for a in range(2):
+        proj_across[a].wait_send()
+        proj_peer[a].wait_send()
+        proj_diag(group, a, 0).wait_send()
+        proj_diag(1 - group, a, 1).wait_send()
+    for k in range(1, n):
+        send_table(k).wait_send()
+    for b in range(n):
+        for s in range(sides):
+            @pl.when(s * 2 + b % 2 != me)
+            def _():
+                att_to(b, s).wait_send()
+
+            to_mate(b, s).wait_send()
+        to_across(b).wait_send()
+        for k in range(1, n):
+            to_row(b, k).wait_send()
+            to_end(b, (me + k) % nt).wait_send()
+    for q in range(2):
+        b = 2 * q + core
+        for k in range(1, n):
+            z_to(b, k).wait_send()
+        for i in range(n):
+            to_across_x(b, i).wait_send()
+            for s in range(sides):
+                to_mate_x(b, s, i).wait_send()
+
+
+def fused(
+    patches, grids, dest, norm_gain, qkv_weight, qkv_bias, proj_weight, proj_bias, merge_gain,
+    w_first, b_first, w_second, seq_rows,
+):
+    n, nt = lax.axis_size("dp"), lax.axis_size("tensor")
+    sides = nt // 2
+    rows, width = patches.shape
+    span = qkv_weight.shape[2]
+    heads = span // HEAD_DIM
+    block = rows // n
+    half = block // sides
+    few = half // 4
+    hidden, columns = w_second.shape
+    wide, lanes = 256, 128
+    pieces = hidden // wide
+    steps = pieces * sides
+    count = n * steps
+    quarter = columns // nt
+    piece = few // 2
+    any_space = pl.BlockSpec(memory_space=pl.ANY)
+    vmem = pl.BlockSpec(memory_space=pltpu.VMEM)
+    smem = pl.BlockSpec(memory_space=pltpu.SMEM)
+    dma = pltpu.SemaphoreType.DMA
+    bf16, f32 = jnp.bfloat16, jnp.float32
+    heads_shape = pltpu.VMEM((heads, rows, lanes), bf16)
+    stack = pltpu.VMEM((count, half, wide), bf16)
+    tiles = pltpu.VMEM((n, 2, block, quarter), bf16)
+    one = pltpu.VMEM((n, block, quarter), bf16)
+    moved = pltpu.VMEM((n, n, n, piece, quarter), bf16)
+    lags = (4, 3, 6, (0, 2, 6, 10))
+    return pl.pallas_call(
+        functools.partial(fused_kernel, seq_rows, lags),
+        out_shape=(
+            jax.ShapeDtypeStruct((n, n, piece, columns), bf16),
+            jax.ShapeDtypeStruct((n, 8, lanes), jnp.int32),
+        ),
+        in_specs=[
+            any_space, smem, vmem, vmem, any_space, vmem, any_space, vmem, vmem, any_space, vmem, any_space],
+        out_specs=(vmem, vmem),
+        scratch_shapes=[
+            pltpu.VMEM((rows, width), bf16),
+            pltpu.VMEM((3, heads * lanes, width), bf16),
+            pltpu.VMEM((3, heads * lanes), f32),
+            pltpu.VMEM((nt, span, width), bf16),
+            pltpu.VMEM((8, rows), jnp.int32),
+            pltpu.VMEM((block, width), bf16),
+            pltpu.VMEM((n, sides, half, width), bf16),
+            heads_shape, heads_shape, heads_shape,
+            pltpu.VMEM((block, span), f32),
+            pltpu.VMEM((n, sides, half, span), bf16),
+            pltpu.VMEM((n // 2, nt, half, span), bf16),
+            pltpu.VMEM((n // 2, n, few, width), bf16),
+            pltpu.VMEM((n, 8, lanes), jnp.int32),
+            pltpu.VMEM((n, sides, n, few, width), bf16),
+            pltpu.VMEM(w_first.shape, bf16),
+            pltpu.VMEM(w_second.shape, bf16),
+            pltpu.VMEM((count, half, wide), f32),
+            stack, stack, stack, stack,
+            pltpu.VMEM((pieces, block, wide), bf16),
+            pltpu.VMEM((2, block, quarter), f32),
+            tiles, tiles, one, one, moved, moved,
+            dma((4,)), dma((3, heads)), dma((n,)), dma((n,)), dma, dma, dma((2,)), dma((2,)), dma((2,)), dma((2,)),
+            dma((2, 2)), dma((2, 2)),
+            dma((n, sides)), dma((n // 2, nt)), dma((n // 2, n)), dma((n // 2, sides, n)), dma((n // 2, n)),
+            dma((n, sides, n)),
+            dma((count,)), dma((count,)), dma((count,)), dma((count,)),
+            dma((n, 2)), dma((n, 2)), dma((n,)), dma((n,)), dma((n, n)), dma((n, n)), dma((n, nt)), dma((n, nt)),
+        ],
+        compiler_params=pltpu.CompilerParams(
+            collective_id=2, has_side_effects=True, vmem_limit_bytes=63 * 1024 * 1024
+        ),
+    )(
+        patches, grids, dest, norm_gain, qkv_weight.swapaxes(1, 2), qkv_bias, proj_weight, proj_bias, merge_gain,
+        w_first, b_first.reshape(pieces, 1, wide), w_second,
+    )
+
+
+def local_fast(
+    patches,
+    grids,
+    dest,
+    norm_gain,
+    qkv_weight,
+    qkv_bias,
+    proj_weight,
+    proj_bias,
+    merge_gain,
+    w_first,
+    b_first,
+    w_second,
+    b_second,
+    text_embed,
+):
+    seq_rows = text_embed.shape[0]
+    visual, arrived = fused(
+        patches, grids, dest, norm_gain, qkv_weight, qkv_bias, proj_weight, proj_bias, merge_gain,
+        w_first, b_first, w_second, seq_rows)
+    visual = visual.reshape(-1, visual.shape[3])
+    arrived_rows = arrived[:, 0, :visual.shape[0] // arrived.shape[0]].reshape(-1)
+    visual = (visual.astype(jnp.float32) + b_second).astype(jnp.bfloat16)
+    hit = jnp.arange(seq_rows, dtype=jnp.int32)[:, None] == arrived_rows[None, :]
+    placed = jnp.dot(hit.astype(jnp.bfloat16), visual, preferred_element_type=jnp.float32).astype(jnp.bfloat16)
+    return jnp.where(jnp.any(hit, axis=1)[:, None], placed, text_embed)
+
+
+def fits(patches, grids, dest, qkv_weight, w_first, w_second):
+    n, nt = lax.axis_size("dp"), lax.axis_size("tensor")
+    rows, width = patches.shape
+    return (
+        n == nt == 4
+        and lax.axis_size("groups") == 2
+        and grids.shape[0] == 1
+        and rows == PATCHES
+        and dest.shape[1] == MERGED
+        and w_first.shape[0] == width
+        and w_second.shape[0] % 256 == 0
+        and w_second.shape[1] % 512 == 0
+        and qkv_weight.shape[2] % 64 == 0
+    )
+
+
+def chosen(*args):
+    run = local_fast if fits(args[0], args[1], args[2], args[4], args[9], args[11]) else local
+    return run(*args)
+
+
 def solution(mesh):
     in_specs = (
         P(("groups", "dp"), None),
@@ -543,4 +1184,4 @@
         P(("groups", "dp"), "tensor"),
     )
     out_specs = P(("groups", "dp"), "tensor")
-    return jax.shard_map(local, mesh=mesh, in_specs=in_specs, out_specs=out_specs, check_vma=False)
+    return jax.shard_map(chosen, mesh=mesh, in_specs=in_specs, out_specs=out_specs, check_vma=False)

time: 289 us -> 158 us (0.55)
  waiting for transfers between devices: 55.1 us -> 0 us
  matrix products: 26 us -> 3.48 us
  blocking collectives: 20.5 us -> 0 us
  between operations: 14.9 us -> 0.01 us
  local copies, waits for them, and re-layouts: 12.5 us -> 2.12 us
  other arithmetic: 7.38 us -> 0.15 us
  starting transfers between devices: 3.32 us -> 0 us
  Pallas kernels: 149 us -> 152 us
    reduce_scatter x1 -> x0, waiting for transfers between devices: 36.5 us -> none  [local(): lax.psum_scatter(partial_value, 'tensor', scatter_dimension=0, tiled=True)]
    all_to_all x1 -> x0, blocking collectives: 20.5 us -> none  [local(): lax.all_to_all(merged_in.reshape(part // 4, dp_count, 4 * width // dp_cou...]
    all_gather x1 -> x0, waiting for transfers between devices: 15.6 us -> none  [local(): received = lax.all_gather(sliced, 'tensor', axis=1, tiled=False)]
    dot_general x4 -> x1, matrix products: 15.1 us -> 3.48 us  [local_fast(): jnp.dot(hit.astype(jnp.bfloat16), visual, preferred_element_type=jnp.floa...]
    sub x1 -> x0, matrix products: 10.9 us -> none  [attention(): exponent = jnp.exp(scores - peak_score)]
    reduce_sum x3 -> x0, other arithmetic: 4.19 us -> none  [the longest x2 4.01 us: rms_scale(): jnp.mean(values * values, axis=-1, keepdims=True) + 1e-06]
    all_gather x1 -> x0, local copies, waits for them, and re-layouts: 3.52 us -> none  [local(): received = lax.all_gather(sliced, 'tensor', axis=1, tiled=False)]
    pallas_call x2 -> x1, Pallas kernels: 149 us -> 152 us  [fused(): pl.pallas_call(functools.partial(fused_kernel, seq_rows, lags), out_shape...]
  transfers between devices with their start and end apart: 3 -> 0, of which waited for: 3 -> 0; matrix products, arithmetic and copies ran while one was open for 1% -> 0% of each run, Pallas kernels for 0% -> 0%
where the time goes in v2:
time: 158 us
  Pallas kernels  152 us (96%)
  matrix products  3.48 us (2%)
  local copies, waits for them, and re-layouts  2.12 us (1%)
    pallas_call x1, Pallas kernels, fused(): pl.pallas_call(functools.partial(fused_kernel, seq_rows, lags), out_shape...  152 us
    dot_general x1, matrix products, local_fast(): jnp.dot(hit.astype(jnp.bfloat16), visual, preferred_element_type=jnp.floa...  3.48 us

profile of v2, /device:TPU:1, one launch (start us, length us, event | category | flops | bytes accessed | tf_op | source)
XLA Modules:
  0.0 157.8 jit_solution(16142604813023349994)
XLA Ops:
  0.0 1.3 reshape.9.bias
  1.3 0.0 copy-start
  1.3 152.1 %shard_map.136 = (bf16[4,4,16,2048]{3,2,1,0:T(8,128)(2,1)}, s32[4,8,128]{2,1,0:T(8,128)}) custom-call(bf16[1024,1280]{1,0:T(8,128)(2,1)} %patches_hbm.1, s32[1,2]{1,0:T(1,128)} %grids.1, s32[1,256]{1,0:T(1,128)} %dest.1, f32[1280]{0:T(1024)} %gain.1, bf16[3,320,1280]{2,1,0:T(8,128)(2,1)} %bitcast.3, f32[3,320]{1,0:T(4,128)} %bqkv.1, ...), custom_call_target="tpu_custom_call" | custom-call | tf_op jit(solution)/shard_map/pallas_call | solution.py:1073
  153.4 0.7 slice_reduce_fusion
  154.1 0.1 eq.16
  154.2 0.2 fusion.4
  154.3 0.0 copy-done
  154.3 3.5 %fusion = bf16[384,2048]{1,0:T(8,128)(2,1)} fusion(bf16[384,2048]{1,0:T(8,128)(2,1)} %param.27, pred[384]{0:T(512)(128)(4,1)S(1)} %fusion.4, bf16[256,2048]{1,0:T(8,128)(2,1)} %bitcast.4, f32[2048]{0:T(1024)S(1)} %copy-done, s32[256]{0:T(256)S(1)} %eq.16), kind=kOutput, calls=%fused_computation.1 | convolution fusion | flops 405897216 | bytes 4203904 | tf_op jit(solution)/shard_map/dot_general | solution.py:1144
Async XLA Ops:
  1.3 153.0 %copy-start = (f32[2048]{0:T(1024)S(1)}, f32[2048]{0:T(1024)}, u32[]{:S(2)}) copy-start(f32[2048]{0:T(1024)} %param.26) | copy-start | bytes 24580

commit v3 on v2

--- a/solution.py
+++ b/solution.py
@@ -528,15 +528,15 @@
 def fused_kernel(
     seq_rows, lags,
     patches_hbm, grids, dest, gain, wqkv_hbm, bqkv, wproj_hbm, bproj, mgain, w1_hbm, bias, w2_hbm,
-    out, arrived,
-    patches, wqkv, bpad, wproj, target, normed, raws, qs, ks, vs, att_f32, att_out, att_in, slices, rows_tbl, x,
+    out, hit_out, any_out,
+    patches, wqkv, bpad, wproj, target, normed, raws, qs, ks, vs, att_f32, att_out, att_in, slices, rows_tbl, arrived, x,
     w1, w2, own, to_r, to_l, from_l, from_r, hidden, keep, give, from_mate, cross, from_across, ready, landed,
     load_sem, head_sem, tbl_send, tbl_recv, pm_send, pm_recv, pa_send, pa_recv, py_send, py_recv, pd_send, pd_recv,
     att_send, att_recv, z_send, fm_send, fa_send, x_recv,
     r_send, r_recv, l_send, l_recv, mate_send, mate_recv, across_send, across_recv,
     row_send, row_recv, end_send, end_recv,
 ):
-    n, sides, _, few, width = x.shape
+    n, _, sides, few, width = x.shape
     nt = 2 * sides
     rows = patches.shape[0]
     block = rows // n
@@ -547,7 +547,8 @@
     count, _, wide = own.shape
     steps = count // n
     pieces = steps // sides
-    quarter = keep.shape[2]
+    pair = n // sides
+    quarter = keep.shape[3]
     piece = ready.shape[3]
     row, me, group = lax.axis_index("dp"), lax.axis_index("tensor"), lax.axis_index("groups")
     core, side = me % 2, me // 2
@@ -577,6 +578,35 @@
     for k in range(1, n):
         pl.semaphore_signal(barrier, inc=1, device_id={"dp": (row + k) % n}, device_id_type=MESH)
     pl.semaphore_signal(barrier, inc=1, device_id={"groups": 1 - group}, device_id_type=MESH)
+
+    live = grids[0, 0] * grids[0, 1]
+    dest_row = dest[...].astype(f32)
+
+    def shards(value):
+        total = jnp.zeros_like(value)
+        for s in range(1, n):
+            total += jnp.where(value >= float(s * seq_rows), 1.0, 0.0)
+        return total
+
+    square = (merged, merged)
+    first_at = lax.broadcasted_iota(jnp.int32, square, 0)
+    second_at = lax.broadcasted_iota(jnp.int32, square, 1)
+    dest_col = jnp.sum(jnp.where(first_at == second_at, dest_row, 0.0), axis=1, keepdims=True)
+    shard_row, shard_col = shards(dest_row), shards(dest_col)
+    rank_col = jnp.sum(
+        jnp.where((shard_row == shard_col) & (second_at < first_at), 1.0, 0.0), axis=1, keepdims=True)
+    live_col = lax.broadcasted_iota(jnp.int32, (merged, 1), 0) * 4 < live
+    rank_i, shard_i = rank_col.astype(jnp.int32), shard_col.astype(jnp.int32)
+    slot_i = rank_i // piece * block + shard_i // 2 * half + shard_i % 2 * piece + rank_i % piece
+    base_col = jnp.where(live_col, slot_i, -rows).astype(f32)
+
+    ones_at = lax.broadcasted_iota(jnp.int32, (1, lanes), 1) == HEAD_DIM
+    for j in range(3):
+        for h in range(heads):
+            bpad[j:j + 1, h * lanes:(h + 1) * lanes] = jnp.where(ones_at, 0.0 if j == 1 else 1.0, 0.0)
+            bpad[j:j + 1, h * lanes:h * lanes + HEAD_DIM] = bqkv[j:j + 1, h * HEAD_DIM:(h + 1) * HEAD_DIM]
+            wqkv[j, h * lanes + HEAD_DIM:(h + 1) * lanes, :] = jnp.zeros((lanes - HEAD_DIM, width), bf16)
+
     pl.semaphore_wait(barrier, nt - 1 + n - 1 + 1)
 
     def remote(source, to, send, recv, device):
@@ -610,29 +640,19 @@
         copy.start()
     proj_mate.start()
 
-    live = grids[0, 0] * grids[0, 1]
-    dest_row = dest[...].astype(f32)
-
-    def shards(value):
-        total = jnp.zeros_like(value)
-        for s in range(1, n):
-            total += jnp.where(value >= float(s * seq_rows), 1.0, 0.0)
-        return total
-
-    square = (merged, merged)
-    first_at = lax.broadcasted_iota(jnp.int32, square, 0)
-    second_at = lax.broadcasted_iota(jnp.int32, square, 1)
-    dest_col = jnp.sum(jnp.where(first_at == second_at, dest_row, 0.0), axis=1, keepdims=True)
-    shard_row, shard_col = shards(dest_row), shards(dest_col)
-    rank_col = jnp.sum(
-        jnp.where((shard_row == shard_col) & (second_at < first_at), 1.0, 0.0), axis=1, keepdims=True)
-    live_col = lax.broadcasted_iota(jnp.int32, (merged, 1), 0) * 4 < live
-    code_col = jnp.where(live_col, shard_col * lanes + rank_col, -1.0)
-    lane_at = lax.broadcasted_iota(jnp.int32, (merged, n * lanes), 1).astype(f32)
+    patch_at = lax.broadcasted_iota(jnp.int32, (1, rows), 1)
+    row4 = lax.broadcasted_iota(jnp.int32, (merged, 1), 0) * 4
+    inside = (patch_at >= row4) & (patch_at < row4 + 4)
+    base_row = jnp.sum(jnp.where(inside, base_col, 0.0), axis=0, keepdims=True).astype(jnp.int32)
+    target[...] = jnp.broadcast_to(base_row + patch_at % 4 * few, target.shape)
+
+    slots = rows_tbl.shape[2]
+    code_col = jnp.where(live_col, shard_col * slots + rank_col + (row * (slots // n)).astype(f32), -1.0)
+    lane_at = lax.broadcasted_iota(jnp.int32, (merged, n * slots), 1).astype(f32)
     local_col = dest_col - shard_col * seq_rows
     table = jnp.sum(jnp.where(lane_at == code_col, local_col + 1.0, 0.0), axis=0, keepdims=True) - 1.0
     for s in range(n):
-        rows_tbl[s] = jnp.broadcast_to(table[:, s * lanes:(s + 1) * lanes], (8, lanes)).astype(jnp.int32)
+        rows_tbl[s] = jnp.broadcast_to(table[:, s * slots:(s + 1) * slots], (8, slots)).astype(jnp.int32)
     arrived[row] = rows_tbl[row]
 
     def send_table(k):
@@ -641,26 +661,6 @@
 
     for k in range(1, n):
         send_table(k).start()
-
-    tall = (merged, rows)
-    at_row = lax.broadcasted_iota(jnp.int32, tall, 0)
-    at_lane = lax.broadcasted_iota(jnp.int32, tall, 1)
-    dest_rep = jnp.sum(jnp.where(at_row == at_lane // 4, dest_col, 0.0), axis=0, keepdims=True)
-    shard_rep = shards(dest_rep)
-    rank_rep = jnp.sum(
-        jnp.where((shard_col == shard_rep) & (at_row < at_lane // 4), 1.0, 0.0), axis=0, keepdims=True)
-    rank_i, shard_i = rank_rep.astype(jnp.int32), shard_rep.astype(jnp.int32)
-    place_i = lax.broadcasted_iota(jnp.int32, (1, rows), 1)
-    slot_i = (
-        rank_i // piece * block + shard_i // 2 * half + place_i % 4 * few + shard_i % 2 * piece + rank_i % piece)
-    target[...] = jnp.broadcast_to(jnp.where(place_i < live, slot_i, -1), target.shape)
-
-    ones_at = lax.broadcasted_iota(jnp.int32, (1, lanes), 1) == HEAD_DIM
-    for j in range(3):
-        for h in range(heads):
-            bpad[j:j + 1, h * lanes:(h + 1) * lanes] = jnp.where(ones_at, 0.0 if j == 1 else 1.0, 0.0)
-            bpad[j:j + 1, h * lanes:h * lanes + HEAD_DIM] = bqkv[j:j + 1, h * HEAD_DIM:(h + 1) * HEAD_DIM]
-            wqkv[j, h * lanes + HEAD_DIM:(h + 1) * lanes, :] = jnp.zeros((lanes - HEAD_DIM, width), bf16)
 
     load_x.wait()
     for load in load_w:
@@ -716,16 +716,23 @@
     def z_to(b, k):
         to = (row + k) % n
         return remote(
-            slices.at[b // 2, to], x.at[b, side, row], z_send.at[b // 2, k], x_recv.at[b, side, row], {"dp": to})
+            slices.at[b // 2, to], x.at[b, row, side], z_send.at[b // 2, k], x_recv.at[b, row, side], {"dp": to})
 
     def to_mate_x(b, s, i):
-        return same(x.at[b, s, i], fm_send.at[b // 2, s, i], x_recv.at[b, s, i], {"tensor": mate})
+        return same(x.at[b, i, s], fm_send.at[b // 2, i, s], x_recv.at[b, i, s], {"tensor": mate})
 
     def to_across_x(b, i):
-        return same(x.at[b, side, i], fa_send.at[b // 2, i], x_recv.at[b, side, i], {"tensor": across})
+        return same(x.at[b, i, side], fa_send.at[b // 2, i], x_recv.at[b, i, side], {"tensor": across})
 
     def x_got(b, s, i):
-        return same(x.at[b, s, i], fm_send.at[b // 2, s, i], x_recv.at[b, s, i], {"tensor": mate})
+        return same(x.at[b, i, s], fm_send.at[b // 2, i, s], x_recv.at[b, i, s], {"tensor": mate})
+
+    def forward(b):
+        for k in range(1, n):
+            source = (row + n - k) % n
+            x_got(b, side, source).wait_recv()
+            to_across_x(b, source).start()
+            to_mate_x(b, side, source).start()
 
     def attend(it, carry):
         @pl.when(it < n)
@@ -762,6 +769,10 @@
                 proj_diag(group, a, 0).wait_recv()
                 proj_diag(1 - group, a, 1).wait_recv()
 
+        @pl.when((it == n - 1) & (core == 0))
+        def _():
+            forward(0)
+
         last = lax.max(it, 1) - 1
 
         @pl.when((it >= 1) & (last % 2 == core))
@@ -776,20 +787,13 @@
                 slices[last // 2, k] = done[k * few:(k + 1) * few, :]
             for k in range(n - 1, 0, -1):
                 z_to(last, k).start()
-            x[last, side, row] = slices[last // 2, row]
+            x[last, row, side] = slices[last // 2, row]
             to_across_x(last, row).start()
             to_mate_x(last, side, row).start()
 
         return carry
 
     lax.fori_loop(0, n + 1, attend, 0)
-
-    def forward(b):
-        for k in range(1, n):
-            source = (row + n - k) % n
-            x_got(b, side, source).wait_recv()
-            to_across_x(b, source).start()
-            to_mate_x(b, side, source).start()
 
     def forward_across(b):
         for k in range(n):
@@ -810,22 +814,22 @@
     def go_left(c):
         return remote(to_l.at[c], from_r.at[c], l_send.at[c], l_recv.at[c], {"dp": left})
 
-    def first(c):
-        b, j = c // steps, c % steps // sides
+    def first(b, j):
         columns = pl.ds(pl.multiple_of(j * wide, wide), wide)
         partial = jnp.dot(x[b].reshape(block, width), w1[:, columns], preferred_element_type=f32)
-        for s in range(sides):
-            own[c + s] = partial[s * half:(s + 1) * half, :]
-
-            @pl.when(row == 0)
-            def _():
-                to_r[c + s] = partial[s * half:(s + 1) * half, :].astype(bf16)
-                go_right(c + s).start()
-
-            @pl.when(row == n - 1)
-            def _():
-                to_l[c + s] = partial[s * half:(s + 1) * half, :].astype(bf16)
-                go_left(c + s).start()
+        for h in range(sides):
+            own[b * steps + h * pieces + j] = partial[h * half:(h + 1) * half, :]
+
+    def begin(c):
+        @pl.when(row == 0)
+        def _():
+            to_r[c] = own[c].astype(bf16)
+            go_right(c).start()
+
+        @pl.when(row == n - 1)
+        def _():
+            to_l[c] = own[c].astype(bf16)
+            go_left(c).start()
 
     def relay(stage, c):
         @pl.when(row == stage)
@@ -841,7 +845,7 @@
             go_left(c).start()
 
     def activate(c):
-        j = c % steps // sides
+        columns = pl.ds(pl.multiple_of(c % pieces * wide, wide), wide)
 
         @pl.when(row == n - 1)
         def _():
@@ -859,9 +863,8 @@
         def _():
             own[c] += from_r[c].astype(f32)
 
-        value = own[c] + bias[j]
-        at = pl.ds(pl.multiple_of(c % sides * half, half), half)
-        hidden[j, at, :] = (0.5 * value * (1.0 + lax.erf(value * math.sqrt(0.5)))).astype(bf16)
+        value = own[c] + bias[columns].reshape(1, wide)
+        hidden[:, columns] = (0.5 * value * (1.0 + lax.erf(value * math.sqrt(0.5)))).astype(bf16)
 
     def columns_of(s, c):
         return pl.ds(pl.multiple_of((s * 2 + c) * quarter, quarter), quarter)
@@ -879,36 +882,35 @@
     def quarter_of(t):
         return pl.ds(pl.multiple_of(t * quarter, quarter), quarter)
 
-    def to_end(b, d):
+    def to_end(g, d):
+        at = pl.ds(g % sides * pair, pair)
         return remote(
-            landed.at[b, d], out.at[:, b, :, quarter_of(me)], end_send.at[b, d], end_recv.at[b, me], {"tensor": d})
-
-    def second(b):
+            landed.at[g, d], out.at[at, g // sides, :, quarter_of(me)], end_send.at[g, d], end_recv.at[g, me],
+            {"tensor": d})
+
+    def second(g):
         def product(columns):
-            acc = jnp.dot(hidden[0], w2[0:wide, columns], preferred_element_type=f32)
-            for j in range(1, pieces):
-                acc += jnp.dot(hidden[j], w2[j * wide:(j + 1) * wide, columns], preferred_element_type=f32)
-            return acc
+            return jnp.dot(hidden[...], w2[:, columns], preferred_element_type=f32)
 
         for s in (1 - side, side):
-            give[b, s] = product(columns_of(s, 1 - core)).astype(bf16)
-            to_mate(b, s).start()
+            give[g, s] = product(columns_of(s, 1 - core)).astype(bf16)
+            to_mate(g, s).start()
         for s in (1 - side, side):
-            keep[s] = product(columns_of(s, core))
+            keep[g % 2, s] = product(columns_of(s, core))
 
     def chip_sum(b):
         to_mate(b, 1 - side).wait_recv()
-        cross[b] = (keep[1 - side] + from_mate[b, 1 - side].astype(f32)).astype(bf16)
+        cross[b] = (keep[b % 2, 1 - side] + from_mate[b, 1 - side].astype(f32)).astype(bf16)
         to_across(b).start()
 
     def spread(b):
         to_mate(b, side).wait_recv()
         to_across(b).wait_recv()
-        value = keep[side] + from_mate[b, side].astype(f32) + from_across[b].astype(f32)
+        value = keep[b % 2, side] + from_mate[b, side].astype(f32) + from_across[b].astype(f32)
         value = value.astype(bf16)
         for s in range(n):
-            for i in range(n):
-                at = s // 2 * half + i * few + s % 2 * piece
+            for i in range(pair):
+                at = (i * n + s) * piece
                 ready[b, s, i] = value[at:at + piece, :]
         for k in range(n - 1, 0, -1):
             to_row(b, k).start()
@@ -924,7 +926,7 @@
 
             @pl.when(source == me)
             def _():
-                out[:, b, :, quarter_of(me)] = landed[b, source]
+                out[pl.ds(b % sides * pair, pair), b // sides, :, quarter_of(me)] = landed[b, source]
 
             @pl.when(source != me)
             def _():
@@ -934,35 +936,50 @@
 
     @pl.when(core == 0)
     def _():
-        forward(0)
         forward_across(0)
 
     @pl.when(core == 1)
     def _():
         forward(1)
 
+    for k in range(1, n):
+        source = (row + n - k) % n
+        remote(rows_tbl.at[0], arrived.at[source], tbl_send.at[0], tbl_recv.at[source], {"dp": source}).wait_recv()
+
+    at_slot = arrived[0, 0:1, :]
+    for i in range(1, n):
+        at_slot = jnp.maximum(at_slot, arrived[i, 0:1, :])
+    match = jnp.where(
+        lax.broadcasted_iota(jnp.int32, hit_out.shape, 0) == at_slot, 1.0, 0.0)
+    hit_out[...] = match.astype(bf16)
+    any_out[...] = jnp.broadcast_to(jnp.max(match, axis=1, keepdims=True), any_out.shape)
+
     load_1.wait()
     load_2.wait()
     after = tuple(zip(offsets, (second, chip_sum, spread, deliver)))
 
     def step(u, carry):
-        @pl.when((u < count) & (u % sides == 0))
+        @pl.when((u < count) & (u % steps < pieces))
         def _():
             @pl.when(u % steps == 0)
             def _():
                 await_x(u // steps)
 
-            first(u)
+            first(u // steps, u % steps)
+
+        @pl.when(u < count)
+        def _():
+            begin(u)
 
         @pl.when((u == 1) & (core == 1))
         def _():
             forward_across(1)
 
-        @pl.when(u == 3)
+        @pl.when(u == 8)
         def _():
             forward(2 + core)
 
-        @pl.when(u == 5)
+        @pl.when(u == 12)
         def _():
             forward_across(2 + core)
 
@@ -978,27 +995,23 @@
             activate(u - lead - fill)
 
         for offset, work in after:
-            late = lead + fill + offset + steps - 1
-
-            @pl.when((u >= late) & (u < count + late) & (lax.max(u - late, 0) % steps == 0))
-            def _():
-                work((u - late) // steps)
+            late = lead + fill + offset + pieces - 1
+
+            @pl.when((u >= late) & (u < count + late) & (lax.max(u - late, 0) % pieces == 0))
+            def _():
+                work((u - late) // pieces)
 
         return carry
 
     lax.fori_loop(0, count + lead + fill + offsets[-1], step, 0)
 
-    for b in range(n):
+    for g in range(n * sides):
         for k in range(1, nt):
             source = (me + k) % nt
             remote(
-                landed.at[b, 0], out.at[:, b, :, quarter_of(source)], end_send.at[b, 0], end_recv.at[b, source],
-                {"tensor": mate},
+                landed.at[g, 0], out.at[g % sides * pair:(g % sides + 1) * pair, g // sides, :, quarter_of(source)],
+                end_send.at[g, 0], end_recv.at[g, source], {"tensor": mate},
             ).wait_recv()
-    for k in range(1, n):
-        source = (row + n - k) % n
-        remote(rows_tbl.at[0], arrived.at[source], tbl_send.at[0], tbl_recv.at[source], {"dp": source}).wait_recv()
-
     def drain(c, carry):
         @pl.when(has_right)
         def _():
@@ -1025,11 +1038,13 @@
             def _():
                 att_to(b, s).wait_send()
 
-            to_mate(b, s).wait_send()
-        to_across(b).wait_send()
+    for g in range(n * sides):
+        for s in range(sides):
+            to_mate(g, s).wait_send()
+        to_across(g).wait_send()
         for k in range(1, n):
-            to_row(b, k).wait_send()
-            to_end(b, (me + k) % nt).wait_send()
+            to_row(g, k).wait_send()
+            to_end(g, (me + k) % nt).wait_send()
     for q in range(2):
         b = 2 * q + core
         for k in range(1, n):
@@ -1066,19 +1081,22 @@
     bf16, f32 = jnp.bfloat16, jnp.float32
     heads_shape = pltpu.VMEM((heads, rows, lanes), bf16)
     stack = pltpu.VMEM((count, half, wide), bf16)
-    tiles = pltpu.VMEM((n, 2, block, quarter), bf16)
-    one = pltpu.VMEM((n, block, quarter), bf16)
-    moved = pltpu.VMEM((n, n, n, piece, quarter), bf16)
-    lags = (4, 3, 6, (0, 2, 6, 10))
+    units = n * sides
+    slots = n * n * piece
+    tiles = pltpu.VMEM((units, 2, half, quarter), bf16)
+    one = pltpu.VMEM((units, half, quarter), bf16)
+    moved = pltpu.VMEM((units, n, n // sides, piece, quarter), bf16)
+    lags = (4, 3, 6, (0, 2, 6, 12))
     return pl.pallas_call(
         functools.partial(fused_kernel, seq_rows, lags),
         out_shape=(
             jax.ShapeDtypeStruct((n, n, piece, columns), bf16),
-            jax.ShapeDtypeStruct((n, 8, lanes), jnp.int32),
+            jax.ShapeDtypeStruct((seq_rows, slots), bf16),
+            jax.ShapeDtypeStruct((seq_rows, lanes), f32),
         ),
         in_specs=[
             any_space, smem, vmem, vmem, any_space, vmem, any_space, vmem, vmem, any_space, vmem, any_space],
-        out_specs=(vmem, vmem),
+        out_specs=(vmem, vmem, vmem),
         scratch_shapes=[
             pltpu.VMEM((rows, width), bf16),
             pltpu.VMEM((3, heads * lanes, width), bf16),
@@ -1092,28 +1110,30 @@
             pltpu.VMEM((n, sides, half, span), bf16),
             pltpu.VMEM((n // 2, nt, half, span), bf16),
             pltpu.VMEM((n // 2, n, few, width), bf16),
-            pltpu.VMEM((n, 8, lanes), jnp.int32),
-            pltpu.VMEM((n, sides, n, few, width), bf16),
+            pltpu.VMEM((n, 8, slots), jnp.int32),
+            pltpu.VMEM((n, 8, slots), jnp.int32),
+            pltpu.VMEM((n, n, sides, few, width), bf16),
             pltpu.VMEM(w_first.shape, bf16),
             pltpu.VMEM(w_second.shape, bf16),
             pltpu.VMEM((count, half, wide), f32),
             stack, stack, stack, stack,
-            pltpu.VMEM((pieces, block, wide), bf16),
-            pltpu.VMEM((2, block, quarter), f32),
+            pltpu.VMEM((half, hidden), bf16),
+            pltpu.VMEM((2, 2, half, quarter), f32),
             tiles, tiles, one, one, moved, moved,
             dma((4,)), dma((3, heads)), dma((n,)), dma((n,)), dma, dma, dma((2,)), dma((2,)), dma((2,)), dma((2,)),
             dma((2, 2)), dma((2, 2)),
-            dma((n, sides)), dma((n // 2, nt)), dma((n // 2, n)), dma((n // 2, sides, n)), dma((n // 2, n)),
-            dma((n, sides, n)),
+            dma((n, sides)), dma((n // 2, nt)), dma((n // 2, n)), dma((n // 2, n, sides)), dma((n // 2, n)),
+            dma((n, n, sides)),
             dma((count,)), dma((count,)), dma((count,)), dma((count,)),
-            dma((n, 2)), dma((n, 2)), dma((n,)), dma((n,)), dma((n, n)), dma((n, n)), dma((n, nt)), dma((n, nt)),
+            dma((units, 2)), dma((units, 2)), dma((units,)), dma((units,)), dma((units, n)), dma((units, n)),
+            dma((units, nt)), dma((units, nt)),
         ],
         compiler_params=pltpu.CompilerParams(
             collective_id=2, has_side_effects=True, vmem_limit_bytes=63 * 1024 * 1024
         ),
     )(
         patches, grids, dest, norm_gain, qkv_weight.swapaxes(1, 2), qkv_bias, proj_weight, proj_bias, merge_gain,
-        w_first, b_first.reshape(pieces, 1, wide), w_second,
+        w_first, b_first, w_second,
     )
 
 
@@ -1134,15 +1154,12 @@
     text_embed,
 ):
     seq_rows = text_embed.shape[0]
-    visual, arrived = fused(
+    visual, hit, taken = fused(
         patches, grids, dest, norm_gain, qkv_weight, qkv_bias, proj_weight, proj_bias, merge_gain,
         w_first, b_first, w_second, seq_rows)
     visual = visual.reshape(-1, visual.shape[3])
-    arrived_rows = arrived[:, 0, :visual.shape[0] // arrived.shape[0]].reshape(-1)
-    visual = (visual.astype(jnp.float32) + b_second).astype(jnp.bfloat16)
-    hit = jnp.arange(seq_rows, dtype=jnp.int32)[:, None] == arrived_rows[None, :]
-    placed = jnp.dot(hit.astype(jnp.bfloat16), visual, preferred_element_type=jnp.float32).astype(jnp.bfloat16)
-    return jnp.where(jnp.any(hit, axis=1)[:, None], placed, text_embed)
+    placed = jnp.dot(hit, visual, preferred_element_type=jnp.float32)
+    return jnp.where(taken[:, :1] > 0.5, (placed + b_second).astype(jnp.bfloat16), text_embed)
 
 
 def fits(patches, grids, dest, qkv_weight, w_first, w_second):

time: 158 us -> 148 us (0.937); the launches traced: 158 us -> 146 us
  Pallas kernels: 152 us -> 141 us
  local copies, waits for them, and re-layouts: 2.12 us -> 0.01 us
    pallas_call x1, Pallas kernels: 152 us -> 141 us  [fused(): pl.pallas_call(functools.partial(fused_kernel, seq_rows, lags), out_shape...]
where the time goes in v3:
time: 148 us; the launch traced here: 146 us
  Pallas kernels  141 us (95%)
  matrix products  3.53 us (2%)
    pallas_call x1, Pallas kernels, fused(): pl.pallas_call(functools.partial(fused_kernel, seq_rows, lags), out_shape...  141 us
    dot_general x1, matrix products, local_fast(): placed = jnp.dot(hit, visual, preferred_element_type=jnp.float32)  3.53 us

profile of v3, /device:TPU:1, one launch (start us, length us, event | category | flops | bytes accessed | tf_op | source)
XLA Modules:
  0.0 145.8 jit_solution(5985490914321899214)
XLA Ops:
  0.0 0.0 copy-start
  0.0 141.1 %shard_map.136 = (bf16[4,4,16,2048]{3,2,1,0:T(8,128)(2,1)}, bf16[384,256]{1,0:T(8,128)(2,1)}, f32[384,128]{1,0:T(8,128)}) custom-call(bf16[1024,1280]{1,0:T(8,128)(2,1)} %patches_hbm.1, s32[1,2]{1,0:T(1,128)} %grids.1, s32[1,256]{1,0:T(1,128)} %dest.1, f32[1280]{0:T(1024)} %gain.1, bf16[3,320,1280]{2,1,0:T(8,128)(2,1)} %bitcast.4, f32[3,320]{1,0:T(4,128)} %bqkv.1, ...), custom_call_target="tpu_custom_call" | custom-call | tf_op jit(solution)/shard_map/pallas_call | solution.py:1090
  141.2 1.1 fusion.1
  142.2 0.0 copy-done
  142.2 3.5 %fusion = bf16[384,2048]{1,0:T(8,128)(2,1)} fusion(bf16[384,2048]{1,0:T(8,128)(2,1)} %param.27, bf16[384,256]{1,0:T(8,128)(2,1)} %get-tuple-element.9, bf16[256,2048]{1,0:T(8,128)(2,1)} %bitcast.5, f32[2048]{0:T(1024)S(1)} %copy-done, pred[384]{0:T(512)(128)(4,1)S(1)} %fusion.1), kind=kOutput, calls=%fused_computation.1 | convolution fusion | flops 405012480 | bytes 4399488 | tf_op jit(solution)/shard_map/dot_general | solution.py:1161
Async XLA Ops:
  0.0 142.2 %copy-start = (f32[2048]{0:T(1024)S(1)}, f32[2048]{0:T(1024)}, u32[]{:S(2)}) copy-start(f32[2048]{0:T(1024)} %param.26) | copy-start | bytes 24580

commit v4 on v3

--- a/solution.py
+++ b/solution.py
@@ -527,9 +527,9 @@
 
 def fused_kernel(
     seq_rows, lags,
-    patches_hbm, grids, dest, gain, wqkv_hbm, bqkv, wproj_hbm, bproj, mgain, w1_hbm, bias, w2_hbm,
-    out, hit_out, any_out,
-    patches, wqkv, bpad, wproj, target, normed, raws, qs, ks, vs, att_f32, att_out, att_in, slices, rows_tbl, arrived, x,
+    patches_hbm, grids, dest, gain, wqkv_hbm, bqkv, wproj_hbm, bproj, mgain, w1_hbm, bias, w2_hbm, bias2, text_hbm,
+    final,
+    patches, wqkv, bpad, wproj, target, normed, raws, qs, ks, vs, att_f32, att_out, att_in, slices, rows_tbl, arrived, hit_out, any_out, out, x,
     w1, w2, own, to_r, to_l, from_l, from_r, hidden, keep, give, from_mate, cross, from_across, ready, landed,
     load_sem, head_sem, tbl_send, tbl_recv, pm_send, pm_recv, pa_send, pa_recv, py_send, py_recv, pd_send, pd_recv,
     att_send, att_recv, z_send, fm_send, fa_send, x_recv,
@@ -549,7 +549,7 @@
     pieces = steps // sides
     pair = n // sides
     quarter = keep.shape[3]
-    piece = ready.shape[3]
+    piece = ready.shape[4]
     row, me, group = lax.axis_index("dp"), lax.axis_index("tensor"), lax.axis_index("groups")
     core, side = me % 2, me // 2
     mate, across = side * 2 + 1 - core, (1 - side) * 2 + core
@@ -561,6 +561,7 @@
     load_p = pltpu.make_async_copy(wproj_hbm, wproj.at[me], load_sem.at[1])
     load_1 = pltpu.make_async_copy(w1_hbm, w1, load_sem.at[2])
     load_2 = pltpu.make_async_copy(w2_hbm, w2, load_sem.at[3])
+    load_t = pltpu.make_async_copy(text_hbm, final, load_sem.at[4])
     load_w = [
         pltpu.make_async_copy(
             wqkv_hbm.at[j, h * HEAD_DIM:(h + 1) * HEAD_DIM], wqkv.at[j, h * lanes:h * lanes + HEAD_DIM],
@@ -578,6 +579,46 @@
     for k in range(1, n):
         pl.semaphore_signal(barrier, inc=1, device_id={"dp": (row + k) % n}, device_id_type=MESH)
     pl.semaphore_signal(barrier, inc=1, device_id={"groups": 1 - group}, device_id_type=MESH)
+
+    pl.semaphore_wait(barrier, nt - 1 + n - 1 + 1)
+
+    def remote(source, to, send, recv, device):
+        return pltpu.make_async_remote_copy(source, to, send, recv, device_id=device, device_id_type=MESH)
+
+    strips = pa_send.shape[0]
+    span = wproj.shape[1] // (2 * strips)
+
+    def strip(g, a):
+        return pl.ds(pl.multiple_of((g * strips + a) * span, span), span)
+
+    def same(ref, send, recv, device):
+        return remote(ref, ref, send, recv, device)
+
+    proj_mate = same(wproj.at[me], pm_send, pm_recv, {"tensor": mate})
+    proj_across = [
+        same(wproj.at[me, strip(group, a)], pa_send.at[a], pa_recv.at[a], {"tensor": across}) for a in range(strips)]
+
+    def proj_got(a):
+        return same(wproj.at[across, strip(group, a)], pa_send.at[a], pa_recv.at[a], {"tensor": across})
+
+    def proj_peer(a):
+        return same(wproj.at[across, strip(group, a)], py_send.at[a], py_recv.at[a], {"groups": 1 - group})
+
+    def proj_peer_got(a):
+        return same(wproj.at[across, strip(1 - group, a)], py_send.at[a], py_recv.at[a], {"groups": 1 - group})
+
+    def proj_diag(g, a, at):
+        return same(wproj.at[across, strip(g, a)], pd_send.at[at, a], pd_recv.at[at, a], {"tensor": mate})
+
+    def proj_pass(a):
+        proj_got(a).wait_recv()
+        proj_peer(a).start()
+        proj_diag(group, a, 0).start()
+
+    load_p.wait()
+    for copy in proj_across:
+        copy.start()
+    proj_mate.start()
 
     live = grids[0, 0] * grids[0, 1]
     dest_row = dest[...].astype(f32)
@@ -607,39 +648,6 @@
             bpad[j:j + 1, h * lanes:h * lanes + HEAD_DIM] = bqkv[j:j + 1, h * HEAD_DIM:(h + 1) * HEAD_DIM]
             wqkv[j, h * lanes + HEAD_DIM:(h + 1) * lanes, :] = jnp.zeros((lanes - HEAD_DIM, width), bf16)
 
-    pl.semaphore_wait(barrier, nt - 1 + n - 1 + 1)
-
-    def remote(source, to, send, recv, device):
-        return pltpu.make_async_remote_copy(source, to, send, recv, device_id=device, device_id_type=MESH)
-
-    span = wproj.shape[1] // 4
-
-    def strip(g, a):
-        return pl.ds(pl.multiple_of((g * 2 + a) * span, span), span)
-
-    def same(ref, send, recv, device):
-        return remote(ref, ref, send, recv, device)
-
-    proj_mate = same(wproj.at[me], pm_send, pm_recv, {"tensor": mate})
-    proj_across = [
-        same(wproj.at[me, strip(group, a)], pa_send.at[a], pa_recv.at[a], {"tensor": across}) for a in range(2)]
-    proj_got = [
-        same(wproj.at[across, strip(group, a)], pa_send.at[a], pa_recv.at[a], {"tensor": across}) for a in range(2)]
-    proj_peer = [
-        same(wproj.at[across, strip(group, a)], py_send.at[a], py_recv.at[a], {"groups": 1 - group})
-        for a in range(2)]
-    proj_peer_got = [
-        same(wproj.at[across, strip(1 - group, a)], py_send.at[a], py_recv.at[a], {"groups": 1 - group})
-        for a in range(2)]
-
-    def proj_diag(g, a, at):
-        return same(wproj.at[across, strip(g, a)], pd_send.at[at, a], pd_recv.at[at, a], {"tensor": mate})
-
-    load_p.wait()
-    for copy in proj_across:
-        copy.start()
-    proj_mate.start()
-
     patch_at = lax.broadcasted_iota(jnp.int32, (1, rows), 1)
     row4 = lax.broadcasted_iota(jnp.int32, (merged, 1), 0) * 4
     inside = (patch_at >= row4) & (patch_at < row4 + 4)
@@ -667,16 +675,12 @@
         load.wait()
     load_1.start()
     load_2.start()
+    load_t.start()
 
     mask_at = lax.broadcasted_iota(jnp.int32, (block, lanes), 1) == HEAD_DIM
 
     def project(b, carry):
-        @pl.when(b == 2)
-        def _():
-            proj_got[0].wait_recv()
-            proj_peer[0].start()
-            proj_diag(group, 0, 0).start()
-
+        proj_pass(b)
         at = pl.ds(pl.multiple_of(b * block, block), block)
         hit = jnp.where(
             target[0:1, :] == lax.broadcasted_iota(jnp.int32, (block, rows), 0) + b * block, 1.0, 0.0)
@@ -697,9 +701,8 @@
 
     lax.fori_loop(0, n, project, 0)
 
-    proj_got[1].wait_recv()
-    proj_peer[1].start()
-    proj_diag(group, 1, 0).start()
+    for a in range(n, strips):
+        proj_pass(a)
 
     scale = math.log2(math.e) / math.sqrt(HEAD_DIM)
 
@@ -759,13 +762,16 @@
                 def _():
                     att_in[b // 2, me] = att_out[b, s]
 
+        @pl.when(it == 0)
+        def _():
+            for a in range(strips):
+                proj_peer_got(a).wait_recv()
+                proj_diag(1 - group, a, 1).start()
+
         @pl.when(it == 1)
         def _():
             proj_mate.wait_recv()
-            for a in range(2):
-                proj_peer_got[a].wait_recv()
-                proj_diag(1 - group, a, 1).start()
-            for a in range(2):
+            for a in range(strips):
                 proj_diag(group, a, 0).wait_recv()
                 proj_diag(1 - group, a, 1).wait_recv()
 
@@ -864,7 +870,7 @@
             own[c] += from_r[c].astype(f32)
 
         value = own[c] + bias[columns].reshape(1, wide)
-        hidden[:, columns] = (0.5 * value * (1.0 + lax.erf(value * math.sqrt(0.5)))).astype(bf16)
+        hidden[c // pieces % 2, :, columns] = (0.5 * value * (1.0 + lax.erf(value * math.sqrt(0.5)))).astype(bf16)
 
     def columns_of(s, c):
         return pl.ds(pl.multiple_of((s * 2 + c) * quarter, quarter), quarter)
@@ -872,65 +878,80 @@
     def to_mate(b, s):
         return remote(give.at[b, s], from_mate.at[b, s], mate_send.at[b, s], mate_recv.at[b, s], {"tensor": mate})
 
-    def to_across(b):
-        return remote(cross.at[b], from_across.at[b], across_send.at[b], across_recv.at[b], {"tensor": across})
-
-    def to_row(b, k):
+    def to_across(g, p):
+        return remote(
+            cross.at[g, p], from_across.at[g, p], across_send.at[g, p], across_recv.at[g, p], {"tensor": across})
+
+    def to_row(g, p, k):
         to = (row + k) % n
-        return remote(ready.at[b, to], landed.at[b, row], row_send.at[b, k], row_recv.at[b, row], {"dp": to})
+        return remote(
+            ready.at[g, p, to], landed.at[g, p, row], row_send.at[g, p, k], row_recv.at[g, p, row], {"dp": to})
 
     def quarter_of(t):
         return pl.ds(pl.multiple_of(t * quarter, quarter), quarter)
 
-    def to_end(g, d):
+    thin = cross.shape[3]
+
+    def columns_in(t, p):
+        return pl.ds(pl.multiple_of(t * quarter + p * thin, thin), thin)
+
+    def to_end(g, p, d):
         at = pl.ds(g % sides * pair, pair)
         return remote(
-            landed.at[g, d], out.at[at, g // sides, :, quarter_of(me)], end_send.at[g, d], end_recv.at[g, me],
-            {"tensor": d})
+            landed.at[g, p, d], out.at[at, g // sides, :, columns_in(me, p)], end_send.at[g, p, d],
+            end_recv.at[g, p, me], {"tensor": d})
+
+    def product(g, s, c):
+        return jnp.dot(hidden[g % 2], w2[:, columns_of(s, c)], preferred_element_type=f32)
 
     def second(g):
-        def product(columns):
-            return jnp.dot(hidden[...], w2[:, columns], preferred_element_type=f32)
-
-        for s in (1 - side, side):
-            give[g, s] = product(columns_of(s, 1 - core)).astype(bf16)
-            to_mate(g, s).start()
-        for s in (1 - side, side):
-            keep[g % 2, s] = product(columns_of(s, core))
-
-    def chip_sum(b):
-        to_mate(b, 1 - side).wait_recv()
-        cross[b] = (keep[b % 2, 1 - side] + from_mate[b, 1 - side].astype(f32)).astype(bf16)
-        to_across(b).start()
-
-    def spread(b):
-        to_mate(b, side).wait_recv()
-        to_across(b).wait_recv()
-        value = keep[b % 2, side] + from_mate[b, side].astype(f32) + from_across[b].astype(f32)
-        value = value.astype(bf16)
-        for s in range(n):
-            for i in range(pair):
-                at = (i * n + s) * piece
-                ready[b, s, i] = value[at:at + piece, :]
-        for k in range(n - 1, 0, -1):
-            to_row(b, k).start()
-        landed[b, row] = ready[b, row]
-
-    def deliver(b):
-        for k in range(n):
-            source = (row + n - k) % n
-            if k:
-                remote(
-                    ready.at[b, 0], landed.at[b, source], row_send.at[b, 0], row_recv.at[b, source], {"dp": left}
-                ).wait_recv()
-
-            @pl.when(source == me)
-            def _():
-                out[pl.ds(b % sides * pair, pair), b // sides, :, quarter_of(me)] = landed[b, source]
-
-            @pl.when(source != me)
-            def _():
-                to_end(b, source).start()
+        give[g, 1 - side] = product(g, 1 - side, 1 - core).astype(bf16)
+        to_mate(g, 1 - side).start()
+        keep[g % 2, 1 - side] = product(g, 1 - side, core)
+
+    def chip_sum(g):
+        to_mate(g, 1 - side).wait_recv()
+        for p in range(2):
+            at = slice(p * thin, (p + 1) * thin)
+            cross[g, p] = (
+                keep[g % 2, 1 - side, :, at] + from_mate[g, 1 - side, :, at].astype(f32)).astype(bf16)
+            to_across(g, p).start()
+        give[g, side] = product(g, side, 1 - core).astype(bf16)
+        to_mate(g, side).start()
+        keep[g % 2, side] = product(g, side, core)
+
+    def spread(g):
+        to_mate(g, side).wait_recv()
+        for p in range(2):
+            at = slice(p * thin, (p + 1) * thin)
+            value = keep[g % 2, side, :, at] + from_mate[g, side, :, at].astype(f32)
+            to_across(g, p).wait_recv()
+            value = (value + from_across[g, p].astype(f32)).astype(bf16)
+            for s in range(n):
+                for i in range(pair):
+                    begin_at = (i * n + s) * piece
+                    ready[g, p, s, i] = value[begin_at:begin_at + piece, :]
+            for k in range(n - 1, 0, -1):
+                to_row(g, p, k).start()
+            landed[g, p, row] = ready[g, p, row]
+
+    def deliver(g):
+        for p in range(2):
+            for k in range(n):
+                source = (row + n - k) % n
+                if k:
+                    remote(
+                        ready.at[g, p, 0], landed.at[g, p, source], row_send.at[g, p, 0],
+                        row_recv.at[g, p, source], {"dp": left},
+                    ).wait_recv()
+
+                @pl.when(source == me)
+                def _():
+                    out[pl.ds(g % sides * pair, pair), g // sides, :, columns_in(me, p)] = landed[g, p, source]
+
+                @pl.when(source != me)
+                def _():
+                    to_end(g, p, source).start()
 
     lead, hop, fill, offsets = lags
 
@@ -956,6 +977,7 @@
 
     load_1.wait()
     load_2.wait()
+    load_t.wait()
     after = tuple(zip(offsets, (second, chip_sum, spread, deliver)))
 
     def step(u, carry):
@@ -1005,13 +1027,25 @@
 
     lax.fori_loop(0, count + lead + fill + offsets[-1], step, 0)
 
-    for g in range(n * sides):
-        for k in range(1, nt):
-            source = (me + k) % nt
-            remote(
-                landed.at[g, 0], out.at[g % sides * pair:(g % sides + 1) * pair, g // sides, :, quarter_of(source)],
-                end_send.at[g, 0], end_recv.at[g, source], {"tensor": mate},
-            ).wait_recv()
+    for k in range(nt):
+        source = (me + k) % nt
+
+        if k:
+            def gather(g, carry):
+                for p in range(2):
+                    remote(
+                        landed.at[g, p, 0],
+                        out.at[pl.ds(g % sides * pair, pair), g // sides, :, columns_in(source, p)],
+                        end_send.at[g, p, 0], end_recv.at[g, p, source], {"tensor": mate},
+                    ).wait_recv()
+                return carry
+
+            lax.fori_loop(0, n * sides, gather, 0)
+        columns = pl.ds(pl.multiple_of(source * quarter, quarter), quarter)
+        rows_in = out[:, :, :, columns].reshape(hit_out.shape[1], quarter)
+        placed = jnp.dot(hit_out[...], rows_in, preferred_element_type=f32) + bias2[columns].reshape(1, quarter)
+        final[:, columns] = jnp.where(any_out[:, 0:1] > 0.5, placed.astype(bf16), final[:, columns])
+
     def drain(c, carry):
         @pl.when(has_right)
         def _():
@@ -1025,9 +1059,9 @@
 
     lax.fori_loop(0, count, drain, 0)
     proj_mate.wait_send()
-    for a in range(2):
+    for a in range(strips):
         proj_across[a].wait_send()
-        proj_peer[a].wait_send()
+        proj_peer(a).wait_send()
         proj_diag(group, a, 0).wait_send()
         proj_diag(1 - group, a, 1).wait_send()
     for k in range(1, n):
@@ -1038,13 +1072,17 @@
             def _():
                 att_to(b, s).wait_send()
 
-    for g in range(n * sides):
-        for s in range(sides):
-            to_mate(g, s).wait_send()
-        to_across(g).wait_send()
-        for k in range(1, n):
-            to_row(g, k).wait_send()
-            to_end(g, (me + k) % nt).wait_send()
+
+    def drain_place(g, carry):
+        for p in range(2):
+            to_mate(g, p).wait_send()
+            to_across(g, p).wait_send()
+            for k in range(1, n):
+                to_row(g, p, k).wait_send()
+                to_end(g, p, (me + k) % nt).wait_send()
+        return carry
+
+    lax.fori_loop(0, n * sides, drain_place, 0)
     for q in range(2):
         b = 2 * q + core
         for k in range(1, n):
@@ -1057,9 +1095,10 @@
 
 def fused(
     patches, grids, dest, norm_gain, qkv_weight, qkv_bias, proj_weight, proj_bias, merge_gain,
-    w_first, b_first, w_second, seq_rows,
+    w_first, b_first, w_second, b_second, text_embed,
 ):
     n, nt = lax.axis_size("dp"), lax.axis_size("tensor")
+    seq_rows = text_embed.shape[0]
     sides = nt // 2
     rows, width = patches.shape
     span = qkv_weight.shape[2]
@@ -1082,21 +1121,19 @@
     heads_shape = pltpu.VMEM((heads, rows, lanes), bf16)
     stack = pltpu.VMEM((count, half, wide), bf16)
     units = n * sides
+    strips = span // 64
     slots = n * n * piece
     tiles = pltpu.VMEM((units, 2, half, quarter), bf16)
-    one = pltpu.VMEM((units, half, quarter), bf16)
-    moved = pltpu.VMEM((units, n, n // sides, piece, quarter), bf16)
-    lags = (4, 3, 6, (0, 2, 6, 12))
+    one = pltpu.VMEM((units, 2, half, quarter // 2), bf16)
+    moved = pltpu.VMEM((units, 2, n, n // sides, piece, quarter // 2), bf16)
+    lags = (4, 3, 6, (0, 1, 6, 12))
     return pl.pallas_call(
         functools.partial(fused_kernel, seq_rows, lags),
-        out_shape=(
-            jax.ShapeDtypeStruct((n, n, piece, columns), bf16),
-            jax.ShapeDtypeStruct((seq_rows, slots), bf16),
-            jax.ShapeDtypeStruct((seq_rows, lanes), f32),
-        ),
+        out_shape=jax.ShapeDtypeStruct(text_embed.shape, bf16),
         in_specs=[
-            any_space, smem, vmem, vmem, any_space, vmem, any_space, vmem, vmem, any_space, vmem, any_space],
-        out_specs=(vmem, vmem, vmem),
+            any_space, smem, vmem, vmem, any_space, vmem, any_space, vmem, vmem, any_space, vmem, any_space, vmem,
+            any_space],
+        out_specs=vmem,
         scratch_shapes=[
             pltpu.VMEM((rows, width), bf16),
             pltpu.VMEM((3, heads * lanes, width), bf16),
@@ -1112,28 +1149,31 @@
             pltpu.VMEM((n // 2, n, few, width), bf16),
             pltpu.VMEM((n, 8, slots), jnp.int32),
             pltpu.VMEM((n, 8, slots), jnp.int32),
+            pltpu.VMEM((seq_rows, slots), bf16),
+            pltpu.VMEM((seq_rows, lanes), f32),
+            pltpu.VMEM((n, n, piece, columns), bf16),
             pltpu.VMEM((n, n, sides, few, width), bf16),
             pltpu.VMEM(w_first.shape, bf16),
             pltpu.VMEM(w_second.shape, bf16),
             pltpu.VMEM((count, half, wide), f32),
             stack, stack, stack, stack,
-            pltpu.VMEM((half, hidden), bf16),
+            pltpu.VMEM((2, half, hidden), bf16),
             pltpu.VMEM((2, 2, half, quarter), f32),
             tiles, tiles, one, one, moved, moved,
-            dma((4,)), dma((3, heads)), dma((n,)), dma((n,)), dma, dma, dma((2,)), dma((2,)), dma((2,)), dma((2,)),
-            dma((2, 2)), dma((2, 2)),
+            dma((5,)), dma((3, heads)), dma((n,)), dma((n,)), dma, dma, dma((strips,)), dma((strips,)), dma((strips,)),
+            dma((strips,)), dma((2, strips)), dma((2, strips)),
             dma((n, sides)), dma((n // 2, nt)), dma((n // 2, n)), dma((n // 2, n, sides)), dma((n // 2, n)),
             dma((n, n, sides)),
             dma((count,)), dma((count,)), dma((count,)), dma((count,)),
-            dma((units, 2)), dma((units, 2)), dma((units,)), dma((units,)), dma((units, n)), dma((units, n)),
-            dma((units, nt)), dma((units, nt)),
+            dma((units, 2)), dma((units, 2)), dma((units, 2)), dma((units, 2)), dma((units, 2, n)), dma((units, 2, n)),
+            dma((units, 2, nt)), dma((units, 2, nt)),
         ],
         compiler_params=pltpu.CompilerParams(
             collective_id=2, has_side_effects=True, vmem_limit_bytes=63 * 1024 * 1024
         ),
     )(
         patches, grids, dest, norm_gain, qkv_weight.swapaxes(1, 2), qkv_bias, proj_weight, proj_bias, merge_gain,
-        w_first, b_first, w_second,
+        w_first, b_first, w_second, b_second, text_embed,
     )
 
 
@@ -1153,13 +1193,9 @@
     b_second,
     text_embed,
 ):
-    seq_rows = text_embed.shape[0]
-    visual, hit, taken = fused(
+    return fused(
         patches, grids, dest, norm_gain, qkv_weight, qkv_bias, proj_weight, proj_bias, merge_gain,
-        w_first, b_first, w_second, seq_rows)
-    visual = visual.reshape(-1, visual.shape[3])
-    placed = jnp.dot(hit, visual, preferred_element_type=jnp.float32)
-    return jnp.where(taken[:, :1] > 0.5, (placed + b_second).astype(jnp.bfloat16), text_embed)
+        w_first, b_first, w_second, b_second, text_embed)
 
 
 def fits(patches, grids, dest, qkv_weight, w_first, w_second):
@@ -1175,6 +1211,7 @@
         and w_second.shape[0] % 256 == 0
         and w_second.shape[1] % 512 == 0
         and qkv_weight.shape[2] % 64 == 0
+        and qkv_weight.shape[2] // 64 > n
     )
 
 

time: 148 us -> 146 us (0.986); the launches traced: 146 us -> 146 us
  matrix products: 3.53 us -> 0 us
  local copies, waits for them, and re-layouts: 0.01 us -> 2.73 us
  Pallas kernels: 141 us -> 143 us
    dot_general x1 -> x0, matrix products: 3.53 us -> none  [local_fast(): placed = jnp.dot(hit, visual, preferred_element_type=jnp.float32)]
    unnamed x2 -> x1, local copies, waits for them, and re-layouts: 0.01 us -> 2.73 us
    pallas_call x1, Pallas kernels: 141 us -> 143 us  [fused(): pl.pallas_call(functools.partial(fused_kernel, seq_rows, lags), out_shape...]
where the time goes in v4:
time: 146 us
  Pallas kernels  143 us (98%)
  local copies, waits for them, and re-layouts  2.73 us (2%)
    pallas_call x1, Pallas kernels, fused(): pl.pallas_call(functools.partial(fused_kernel, seq_rows, lags), out_shape...  143 us

profile of v4, /device:TPU:1, one launch (start us, length us, event | category | flops | bytes accessed | tf_op | source)
XLA Modules:
  0.0 146.0 jit_solution(16128397801970052855)
XLA Ops:
  0.0 143.3 %shard_map.136 = bf16[384,2048]{1,0:T(8,128)(2,1)} custom-call(bf16[1024,1280]{1,0:T(8,128)(2,1)} %patches_hbm.1, s32[1,2]{1,0:T(1,128)} %grids.1, s32[1,256]{1,0:T(1,128)} %dest.1, f32[1280]{0:T(1024)} %gain.1, bf16[3,320,1280]{2,1,0:T(8,128)(2,1)} %bitcast.1, f32[3,320]{1,0:T(4,128)} %bqkv.1, bf16[320,1280]{1,0:T(8,128)(2,1)} %wproj_hbm.1, f32[1280]{0:T(1024)} %bproj.1, ...), custom_call_target="tpu_custom_call" | custom-call | tf_op jit(solution)/shard_map/pallas_call | solution.py:1130
  143.3 2.7 %copy.16 = bf16[384,2048]{1,0:T(8,128)(2,1)} copy(bf16[384,2048]{1,0:T(8,128)(2,1)} %shard_map.136) | data formatting | bytes 3145728

commit v5 on v4

--- a/solution.py
+++ b/solution.py
@@ -680,7 +680,10 @@
     mask_at = lax.broadcasted_iota(jnp.int32, (block, lanes), 1) == HEAD_DIM
 
     def project(b, carry):
-        proj_pass(b)
+        @pl.when(b >= 1)
+        def _():
+            proj_pass(lax.max(b, 1) - 1)
+
         at = pl.ds(pl.multiple_of(b * block, block), block)
         hit = jnp.where(
             target[0:1, :] == lax.broadcasted_iota(jnp.int32, (block, rows), 0) + b * block, 1.0, 0.0)
@@ -701,8 +704,7 @@
 
     lax.fori_loop(0, n, project, 0)
 
-    for a in range(n, strips):
-        proj_pass(a)
+    proj_pass(n - 1)
 
     scale = math.log2(math.e) / math.sqrt(HEAD_DIM)
 
@@ -764,12 +766,17 @@
 
         @pl.when(it == 0)
         def _():
-            for a in range(strips):
+            for a in range(n, strips):
+                proj_pass(a)
+            for a in range(n):
                 proj_peer_got(a).wait_recv()
                 proj_diag(1 - group, a, 1).start()
 
         @pl.when(it == 1)
         def _():
+            for a in range(n, strips):
+                proj_peer_got(a).wait_recv()
+                proj_diag(1 - group, a, 1).start()
             proj_mate.wait_recv()
             for a in range(strips):
                 proj_diag(group, a, 0).wait_recv()

time: 146 us -> 144 us (0.986)
  Pallas kernels: 143 us -> 141 us
    pallas_call x1, Pallas kernels: 143 us -> 141 us  [fused(): pl.pallas_call(functools.partial(fused_kernel, seq_rows, lags), out_shape...]
where the time goes in v5:
time: 144 us
  Pallas kernels  141 us (98%)
  local copies, waits for them, and re-layouts  2.73 us (2%)
    pallas_call x1, Pallas kernels, fused(): pl.pallas_call(functools.partial(fused_kernel, seq_rows, lags), out_shape...  141 us

profile of v5, /device:TPU:1, one launch (start us, length us, event | category | flops | bytes accessed | tf_op | source)
XLA Modules:
  0.0 144.1 jit_solution(3937532059863106624)
XLA Ops:
  0.0 141.4 %shard_map.136 = bf16[384,2048]{1,0:T(8,128)(2,1)} custom-call(bf16[1024,1280]{1,0:T(8,128)(2,1)} %patches_hbm.1, s32[1,2]{1,0:T(1,128)} %grids.1, s32[1,256]{1,0:T(1,128)} %dest.1, f32[1280]{0:T(1024)} %gain.1, bf16[3,320,1280]{2,1,0:T(8,128)(2,1)} %bitcast.1, f32[3,320]{1,0:T(4,128)} %bqkv.1, bf16[320,1280]{1,0:T(8,128)(2,1)} %wproj_hbm.1, f32[1280]{0:T(1024)} %bproj.1, ...), custom_call_target="tpu_custom_call" | custom-call | tf_op jit(solution)/shard_map/pallas_call | solution.py:1137
  141.4 2.7 %copy.16 = bf16[384,2048]{1,0:T(8,128)(2,1)} copy(bf16[384,2048]{1,0:T(8,128)(2,1)} %shard_map.136) | data formatting | bytes 3145728
